TPU v7x, 128 devices: a whole 4x4x4 slice. The times are simulated.
128 devices in a mesh: prob: 1, samp: 16 (over z, y), feat: 8 (over x, core).
Axes of the slice: x: 4, y: 4, z: 4, core: 2. Of those that a mesh axis runs over, the one named last changes fastest.
Arguments:
- x_mat: bfloat16 [8192, 16384], P(('prob', 'samp'), 'feat')
- w_init: float32 [16384, 256], P(('prob', 'feat'))
- targets: float32 [8192, 256], P(('prob', 'samp'))
- step_size: float32 [16384], P(('prob', 'feat'))
Outputs:
- output 1: float32 [16384, 256], P(('prob', 'feat'))
- output 2: float32 [8192, 256], P(('prob', 'samp'))
All inputs are finite; a program needn't handle non-finite values.
Results may differ from a plain program's by a relative error of at most 0.0040641.
Values are sent between devices in bfloat16 or wider.
A program may use at most 1 GiB of HBM per device.

v0:
```python
import jax
import jax.numpy as jnp
from jax import lax
from jax.sharding import PartitionSpec as P, NamedSharding

SWEEPS = 4
COMBINE_WEIGHT = 0.8
RIDGE_SCALE = 0.1


def solution(mesh):
    samp_count = mesh.shape["samp"]
    feat_count = mesh.shape["feat"]

    def local_solve(x_loc, w_loc, y_loc, eta_loc):
        rows_loc, feat_len = x_loc.shape
        samples = rows_loc * samp_count
        ridge = RIDGE_SCALE * (feat_len * feat_count) / samples
        first = jnp.dot(x_loc, w_loc.astype(jnp.bfloat16), preferred_element_type=jnp.float32)
        residual = y_loc - lax.psum(first.astype(jnp.bfloat16).astype(jnp.float32), "feat")
        weights = w_loc
        for sweep in range(SWEEPS):
            part_grad = lax.dot_general(x_loc, residual.astype(jnp.bfloat16), (((0,), (0,)), ((), ())), preferred_element_type=jnp.float32)
            gradient = lax.psum(part_grad, "samp") / samples
            delta = eta_loc[:, None] * (gradient - ridge * weights)
            weights = weights + COMBINE_WEIGHT * delta
            update = jnp.dot(x_loc, delta.astype(jnp.bfloat16), preferred_element_type=jnp.float32)
            residual = residual - COMBINE_WEIGHT * lax.psum(update.astype(jnp.bfloat16).astype(jnp.float32), "feat")
        return weights, residual

    return jax.shard_map(
        local_solve,
        mesh=mesh,
        in_specs=(P(("prob", "samp"), "feat"), P(("prob", "feat"), None), P(("prob", "samp"), None), P(("prob", "feat"))),
        out_specs=(P(("prob", "feat"), None), P(("prob", "samp"), None)),
        check_vma=False,
    )
```

profile of v0, /device:TPU:1, one launch (start us, length us, event | category | flops | bytes accessed | tf_op | source)
XLA Modules:
  0.0 713.9 jit_solution(11963612520771605697)
XLA Ops:
  7.2 0.0 copy-start
  7.2 0.0 all-reduce.10.cloned.1.call-start
  7.2 1.5 copy-done
  8.8 3.1 fusion.4
  11.9 0.0 all-reduce.10.cloned.1.call-update
  11.9 0.0 all-reduce.12.cloned.1.call-start
  11.9 62.0 %all-reduce.10.cloned.1.call-done = f32[512,256]{1,0:T(8,128)} async-done(((f32[512,256]{1,0:T(8,128)}), f32[512,256]{1,0:T(8,128)}) %all-reduce.10.cloned.1.call-update) | async-done | bytes 524304 | tf_op jit(solution)/shard_map/psum | solution.py:20
  74.0 0.0 copy-done.2
  74.0 1.1 sub.27
  75.1 2.0 convolution_bitcast_fusion.3
  77.1 0.0 all-reduce.12.cloned.1.call-update
  77.1 0.0 copy-start.3
  77.2 0.0 all-reduce.14.cloned.1.call-start
  77.2 2.9 copy.7
  80.1 87.9 %all-reduce.12.cloned.1.call-done = f32[2048,256]{0,1:T(8,128)} async-done(((f32[2048,256]{0,1:T(8,128)}), f32[2048,256]{0,1:T(8,128)}) %all-reduce.12.cloned.1.call-update) | async-done | bytes 2097168 | tf_op jit(solution)/shard_map/psum | solution.py:24
  168.0 0.0 copy-done.3
  168.0 3.8 fusion.6
  171.8 0.0 all-reduce.14.cloned.1.call-update
  171.8 0.0 all-reduce.16.cloned.1.call-start
  171.9 59.5 %all-reduce.14.cloned.1.call-done = f32[512,256]{1,0:T(8,128)} async-done(((f32[512,256]{1,0:T(8,128)}), f32[512,256]{1,0:T(8,128)}) %all-reduce.14.cloned.1.call-update) | async-done | bytes 524304 | tf_op jit(solution)/shard_map/psum | solution.py:28
  231.3 3.1 convolution_bitcast_fusion.2
  234.4 0.0 all-reduce.16.cloned.1.call-update
  234.5 0.0 all-reduce.18.cloned.1.call-start
  234.5 90.8 %all-reduce.16.cloned.1.call-done = f32[2048,256]{0,1:T(8,128)} async-done(((f32[2048,256]{0,1:T(8,128)}), f32[2048,256]{0,1:T(8,128)}) %all-reduce.16.cloned.1.call-update) | async-done | bytes 2097168 | tf_op jit(solution)/shard_map/psum | solution.py:24
  325.3 4.7 fusion.8
  330.0 0.0 all-reduce.18.cloned.1.call-update
  330.0 0.0 all-reduce.20.cloned.1.call-start
  330.1 59.5 %all-reduce.18.cloned.1.call-done = f32[512,256]{1,0:T(8,128)} async-done(((f32[512,256]{1,0:T(8,128)}), f32[512,256]{1,0:T(8,128)}) %all-reduce.18.cloned.1.call-update) | async-done | bytes 524304 | tf_op jit(solution)/shard_map/psum | solution.py:28
  389.5 1.3 multiply_subtract_fusion.2
  390.8 2.1 convolution_bitcast_fusion.1
  392.9 0.0 all-reduce.20.cloned.1.call-update
  392.9 0.0 all-reduce.22.cloned.1.call-start
  393.0 5.1 multiply_add_fusion.2
  398.1 85.7 %all-reduce.20.cloned.1.call-done = f32[2048,256]{0,1:T(8,128)} async-done(((f32[2048,256]{0,1:T(8,128)}), f32[2048,256]{0,1:T(8,128)}) %all-reduce.20.cloned.1.call-update) | async-done | bytes 2097168 | tf_op jit(solution)/shard_map/psum | solution.py:24
  483.8 3.8 fusion.10
  487.6 0.0 all-reduce.22.cloned.1.call-update
  487.6 0.0 all-reduce.24.cloned.1.call-start
  487.7 59.5 %all-reduce.22.cloned.1.call-done = f32[512,256]{1,0:T(8,128)} async-done(((f32[512,256]{1,0:T(8,128)}), f32[512,256]{1,0:T(8,128)}) %all-reduce.22.cloned.1.call-update) | async-done | bytes 524304 | tf_op jit(solution)/shard_map/psum | solution.py:28
  547.1 3.1 convolution_bitcast_fusion
  550.2 0.0 all-reduce.24.cloned.1.call-update
  550.3 0.0 all-reduce.26.cloned.1.call-start
  550.3 90.8 %all-reduce.24.cloned.1.call-done = f32[2048,256]{0,1:T(8,128)} async-done(((f32[2048,256]{0,1:T(8,128)}), f32[2048,256]{0,1:T(8,128)}) %all-reduce.24.cloned.1.call-update) | async-done | bytes 2097168 | tf_op jit(solution)/shard_map/psum | solution.py:24
  641.1 4.7 fusion.12
  645.9 0.0 all-reduce.26.cloned.1.call-update
  645.9 5.1 multiply_add_fusion
  651.0 2.9 copy.12
  654.0 51.4 %all-reduce.26.cloned.1.call-done = f32[512,256]{1,0:T(8,128)} async-done(((f32[512,256]{1,0:T(8,128)}), f32[512,256]{1,0:T(8,128)}) %all-reduce.26.cloned.1.call-update) | async-done | bytes 524304 | tf_op jit(solution)/shard_map/psum | solution.py:28
  705.4 1.9 multiply_subtract_fusion
  (3 shorter events, 0.0 us)
Async XLA Ops:
  7.2 1.6 copy-start
  7.2 66.8 %copy-start.2 = (f32[512,256]{1,0:T(8,128)S(1)}, f32[512,256]{1,0:T(8,128)}, u32[]{:S(2)}) copy-start(f32[512,256]{1,0:T(8,128)} %param.6) | copy-start | bytes 1572868
  7.2 66.8 %all-reduce.10.cloned.1.call-start = ((), (), s32[]{:S(2)}) async-start(), calls=%async_computation | async-start | bytes 1048576 | tf_op jit(solution)/shard_map/psum | solution.py:20
  11.9 156.1 %all-reduce.12.cloned.1.call-start = ((), (), s32[]{:S(2)}) async-start(), calls=%async_computation.1 | async-start | bytes 4194304 | tf_op jit(solution)/shard_map/psum | solution.py:24
  77.1 90.8 %copy-start.3 = (f32[2048]{0:T(1024)S(1)}, f32[2048]{0:T(1024)}, u32[]{:S(2)}) copy-start(f32[2048]{0:T(1024)} %param.7) | copy-start | bytes 24580
  77.2 154.2 %all-reduce.14.cloned.1.call-start = ((), (), s32[]{:S(2)}) async-start(), calls=%async_computation.2 | async-start | bytes 1048576 | tf_op jit(solution)/shard_map/psum | solution.py:28
  171.8 153.5 %all-reduce.16.cloned.1.call-start = ((), (), s32[]{:S(2)}) async-start(), calls=%async_computation.3 | async-start | bytes 4194304 | tf_op jit(solution)/shard_map/psum | solution.py:24
  234.5 155.1 %all-reduce.18.cloned.1.call-start = ((), (), s32[]{:S(2)}) async-start(), calls=%async_computation.4 | async-start | bytes 1048576 | tf_op jit(solution)/shard_map/psum | solution.py:28
  330.0 153.7 %all-reduce.20.cloned.1.call-start = ((), (), s32[]{:S(2)}) async-start(), calls=%async_computation.5 | async-start | bytes 4194304 | tf_op jit(solution)/shard_map/psum | solution.py:24
  392.9 154.2 %all-reduce.22.cloned.1.call-start = ((), (), s32[]{:S(2)}) async-start(), calls=%async_computation.6 | async-start | bytes 1048576 | tf_op jit(solution)/shard_map/psum | solution.py:28
  487.6 153.5 %all-reduce.24.cloned.1.call-start = ((), (), s32[]{:S(2)}) async-start(), calls=%async_computation.7 | async-start | bytes 4194304 | tf_op jit(solution)/shard_map/psum | solution.py:24
  550.3 155.1 %all-reduce.26.cloned.1.call-start = ((), (), s32[]{:S(2)}) async-start(), calls=%async_computation.8 | async-start | bytes 1048576 | tf_op jit(solution)/shard_map/psum | solution.py:28
  651.0 54.4 %copy-start.1 = (f32[512,256]{1,0:T(8,128)S(1)}, f32[512,256]{1,0:T(8,128)}, u32[]{:S(2)}) copy-start(f32[512,256]{1,0:T(8,128)} %all-reduce.22.cloned.1.call-done) | copy-start | bytes 1572868
Sparse Core Ops, SparseCore 0:
  12.0 61.9 all-reduce.9
  77.3 90.6 all-reduce.11
  172.0 59.3 all-reduce.13
  234.6 90.6 all-reduce.15
  330.1 59.3 all-reduce.17
  393.1 90.6 all-reduce.19
  487.7 59.3 all-reduce.21
  550.5 90.6 all-reduce.23
  646.0 59.3 all-reduce.25
where the time goes:
time: 716 us; the launch traced here: 714 us
  waiting for transfers between devices  647 us (90%)
  matrix products  30.5 us (4%)
  other arithmetic  14.6 us (2%)
  between operations  13.9 us (2%)
  local copies, waits for them, and re-layouts  7.37 us (1%)
    psum x4, waiting for transfers between devices, local_solve(): gradient = lax.psum(part_grad, 'samp') / samples  355 us
    psum x4, waiting for transfers between devices, local_solve(): lax.psum(update.astype(jnp.bfloat16).astype(jnp.float32), 'feat')  230 us
    psum x1, waiting for transfers between devices, local_solve(): lax.psum(first.astype(jnp.bfloat16).astype(jnp.float32), 'feat')  62 us
    dot_general x4, matrix products, local_solve(): jnp.dot(x_loc, delta.astype(jnp.bfloat16), preferred_element_type=jnp.flo...  17.1 us
  transfers between devices with their start and end apart: 9, of which 9 were waited for; matrix products, arithmetic and copies ran while one was open for 2% of the time, Pallas kernels for 0%

commit v1 on v0

v1 whole, which is shorter than its diff:
```python
import functools
import math

import jax
import jax.numpy as jnp
from jax import lax
from jax.experimental import pallas as pl
from jax.experimental.pallas import tpu as pltpu
from jax.sharding import PartitionSpec as P

SWEEPS = 4
COMBINE_WEIGHT = 0.8
RIDGE_SCALE = 0.1
PARTS = 2
LANES = 128
MESH = pl.DeviceIdType.MESH
F32 = jnp.float32
BF16 = jnp.bfloat16


def ridge_kernel(ring, chips, samples, ridge, x_hbm, w_hbm, y_hbm, eta_hbm, wo_hbm, ro_hbm,
                 x, xt, w_in, w, r, eta_in, eta_t, eta, g, rs1, s1, rs2, dw, u, ur, rb, wo, ro,
                 load_sem, store_sem,
                 rs1_s, rs1_r, rs2_s, rs2_r, ag1_s, ag1_r, ag2_s, ag2_r,
                 u_s, u_r, rg_s, rg_r, wg1_s, wg1_r, wg2_s, wg2_r, rf_s, rf_r):
    samp = lax.axis_index("samp")
    feat = lax.axis_index("feat")
    rows, width = x.shape
    half = width // 2
    group = half // ring
    chunk = group // ring
    piece = rows // (2 * chips)
    cy, cz = lax.rem(samp, ring), lax.div(samp, ring)
    cx, core = lax.div(feat, 2), lax.rem(feat, 2)
    ys = [cy] + [lax.rem(cy + d, ring) for d in range(1, ring)]
    zs = [cz] + [lax.rem(cz + d, ring) for d in range(1, ring)]
    firsts = (ys, zs)
    seconds = (zs, ys)
    neighbour = [[cz * ring + c for c in ys], [c * ring + cy for c in zs]]
    far_first = sorted(range(1, ring), key=lambda d: -min(d, ring - d))
    peers = [(dx, dc) for dx in far_first + [0] for dc in (0, 1) if dx or dc]

    xs = [cx] + [lax.rem(cx + d, chips) for d in range(1, chips)]
    cores = [core, 1 - core]
    feats = [xs[dx] * 2 + cores[dc] for dx, dc in peers]
    group_rows = [[h * half + c * group for c in firsts[h]] for h in (0, 1)]
    chunk_rows = [[c * chunk for c in seconds[h]] for h in (0, 1)]
    own_chunks = [[group_rows[h][0] + c for c in chunk_rows[h]] for h in (0, 1)]
    piece_rows = [f * piece for f in feats]
    mine = pl.ds(feat * piece, piece)

    def along(axis, d):
        return {"samp": neighbour[axis][d]}

    def remote(src, dst, send, recv, device):
        return pltpu.make_async_remote_copy(
            src_ref=src, dst_ref=dst, send_sem=send, recv_sem=recv, device_id=device, device_id_type=MESH)

    def group_at(h, d):
        return pl.ds(group_rows[h][d], group)

    def part_at(h, e):
        return pl.ds(chunk_rows[h][e], chunk)

    def chunk_at(h, e):
        return pl.ds(own_chunks[h][e], chunk)

    def rs1_copy(p, h, d):
        return remote(g.at[p, group_at(h, d)], rs1.at[p, h, d - 1],
                      rs1_s.at[p, h, d - 1], rs1_r.at[p, h, d - 1], along(h, d))

    def rs2_copy(p, h, d):
        return remote(s1.at[p, h, part_at(h, d)], rs2.at[p, h, d - 1],
                      rs2_s.at[p, h, d - 1], rs2_r.at[p, h, d - 1], along(1 - h, d))

    def gather1(buf, ss, rr, p, h, d):
        at = chunk_at(h, 0)
        return remote(buf.at[p, at], buf.at[p, at], ss.at[p, h, d - 1], rr.at[p, h, d - 1], along(1 - h, d))

    def gather2(buf, ss, rr, p, h, e, d):
        at = chunk_at(h, (ring - e) % ring)
        return remote(buf.at[p, at], buf.at[p, at], ss.at[p, h, e, d - 1], rr.at[p, h, e, d - 1], along(h, d))

    def u_copy(p, i):
        return remote(u.at[p, pl.ds(piece_rows[i], piece)], ur.at[p, i], u_s.at[p, i], u_r.at[p, i], {"feat": feats[i]})

    def r_copy(buf, ss, rr, p, i):
        return remote(buf.at[p, mine], buf.at[p, mine], ss.at[p, i], rr.at[p, i], {"feat": feats[i]})

    def start_u(p):
        step = max(rows // 2, piece)
        for k in range(rows // step):
            at = pl.ds(k * step, step)
            u[p, at] = jnp.dot(x[at], dw[p], preferred_element_type=F32).astype(BF16)
        for i in range(len(peers)):
            u_copy(p, i).start()

    def sum_u(p):
        total = u[p, mine].astype(F32)
        for i in range(len(peers)):
            u_copy(p, i).wait_recv()
        for i in range(len(peers)):
            total = total + ur[p, i].astype(F32)
        for i in range(len(peers)):
            u_copy(p, i).wait_send()
        return total

    def send_r(p):
        rb[p, mine] = r[p].astype(BF16)
        for i in range(len(peers)):
            r_copy(rb, rg_s, rg_r, p, i).start()

    def start_g(p):
        for i in range(len(peers)):
            r_copy(rb, rg_s, rg_r, p, i).wait_recv()
        for d in far_first + [0]:
            for h in (0, 1):
                at = group_at(h, d)
                g[p, at] = jnp.dot(xt[at], rb[p], preferred_element_type=F32)
                if d:
                    rs1_copy(p, h, d).start()
        for i in range(len(peers)):
            r_copy(rb, rg_s, rg_r, p, i).wait_send()

    def mid_g(p):
        for h in (0, 1):
            for d in range(1, ring):
                rs1_copy(p, h, d).wait_recv()
            for e in far_first + [0]:
                total = g[p, chunk_at(h, e)]
                for d in range(1, ring):
                    total = total + rs1[p, h, d - 1, part_at(h, e)]
                s1[p, h, part_at(h, e)] = total
                if e:
                    rs2_copy(p, h, e).start()

    def end_g(p, last):
        for h in (0, 1):
            for d in range(1, ring):
                rs2_copy(p, h, d).wait_recv()
            total = s1[p, h, part_at(h, 0)]
            for d in range(1, ring):
                total = total + rs2[p, h, d - 1]
            delta = eta[h] * (total / samples - ridge * w[p, h])
            at = chunk_at(h, 0)
            dw[p, at] = delta.astype(BF16)
            for d in far_first:
                gather1(dw, ag1_s, ag1_r, p, h, d).start()
            for d in far_first:
                gather2(dw, ag2_s, ag2_r, p, h, 0, d).start()
            new = w[p, h] + COMBINE_WEIGHT * delta
            w[p, h] = new
            if last:
                wo[p, at] = new

    def relay(buf, s1_, r1_, s2_, r2_, p):
        for e in range(1, ring):
            for h in (0, 1):
                gather1(buf, s1_, r1_, p, h, e).wait_recv()
                for d in far_first:
                    gather2(buf, s2_, r2_, p, h, e, d).start()

    def gathered(buf, s1_, r1_, s2_, r2_, p):
        for h in (0, 1):
            for e in range(ring):
                for d in range(1, ring):
                    gather2(buf, s2_, r2_, p, h, e, d).wait_recv()
        for h in (0, 1):
            for d in range(1, ring):
                gather1(buf, s1_, r1_, p, h, d).wait_send()
                for e in range(ring):
                    gather2(buf, s2_, r2_, p, h, e, d).wait_send()

    def sent_g(p):
        for h in (0, 1):
            for d in range(1, ring):
                rs1_copy(p, h, d).wait_send()
                rs2_copy(p, h, d).wait_send()

    ag = (dw, ag1_s, ag1_r, ag2_s, ag2_r)
    wg = (wo, wg1_s, wg1_r, wg2_s, wg2_r)

    loads = [pltpu.make_async_copy(w_hbm, w_in, load_sem.at[0]),
             pltpu.make_async_copy(x_hbm, x, load_sem.at[1]),
             pltpu.make_async_copy(eta_hbm, eta_in, load_sem.at[2])]
    loads += [pltpu.make_async_copy(y_hbm.at[mine, pl.ds(p * LANES, LANES)], r.at[p], load_sem.at[3 + p])
              for p in range(PARTS)]
    for load in loads:
        load.start()
    barrier = pltpu.get_barrier_semaphore()
    for d in range(1, ring):
        for axis in (0, 1):
            pl.semaphore_signal(barrier, inc=1, device_id=along(axis, d), device_id_type=MESH)
    for i in range(len(peers)):
        pl.semaphore_signal(barrier, inc=1, device_id={"feat": feats[i]}, device_id_type=MESH)
    loads[0].wait()
    for p in range(PARTS):
        dw[p] = w_in[:, p * LANES:(p + 1) * LANES].astype(BF16)
        for h in (0, 1):
            w[p, h] = w_in[chunk_at(h, 0), p * LANES:(p + 1) * LANES]
    loads[1].wait()
    pl.semaphore_wait(barrier, 2 * (ring - 1) + len(peers))

    for p in range(PARTS):
        start_u(p)
    tile = min(width, 256)
    for k in range(width // tile):
        at = pl.ds(k * tile, tile)
        xt[at] = x[:, k * tile:(k + 1) * tile].T
    loads[2].wait()
    for h in (0, 1):
        pos = own_chunks[h][0]
        line = eta_in[pl.ds(lax.div(pos, LANES), 1), :]
        wide = jnp.broadcast_to(line, (LANES, LANES)).T
        eta_t[...] = wide
        eta[h] = eta_t[pl.ds(lax.rem(pos, LANES), chunk), :]
    for p in range(PARTS):
        loads[3 + p].wait()
        r[p] = r[p] - sum_u(p)
        send_r(p)

    def sweep(last):
        for p in range(PARTS):
            start_g(p)
        for p in range(PARTS):
            mid_g(p)
        for p in range(PARTS):
            end_g(p, last)
        for p in range(PARTS):
            relay(*ag, p)
        if last:
            for p in range(PARTS):
                for h in (0, 1):
                    for d in far_first:
                        gather1(*wg[:3], p, h, d).start()
                    for d in far_first:
                        gather2(wo, wg2_s, wg2_r, p, h, 0, d).start()
        for p in range(PARTS):
            sent_g(p)
            gathered(*ag, p)
            start_u(p)
        if last:
            for p in range(PARTS):
                relay(*wg, p)
        for p in range(PARTS):
            r[p] = r[p] - COMBINE_WEIGHT * sum_u(p)
            if last:
                ro[p, mine] = r[p]
                for i in range(len(peers)):
                    r_copy(ro, rf_s, rf_r, p, i).start()
            else:
                send_r(p)

    def body(i, carry):
        sweep(False)
        return carry

    lax.fori_loop(0, SWEEPS - 1, body, 0)
    sweep(True)

    stores = []
    for p in range(PARTS):
        for i in range(len(peers)):
            r_copy(ro, rf_s, rf_r, p, i).wait_recv()
        stores.append(pltpu.make_async_copy(ro.at[p], ro_hbm.at[:, pl.ds(p * LANES, LANES)], store_sem.at[p]))
        stores[-1].start()
    for p in range(PARTS):
        gathered(*wg, p)
        stores.append(pltpu.make_async_copy(wo.at[p], wo_hbm.at[:, pl.ds(p * LANES, LANES)], store_sem.at[PARTS + p]))
        stores[-1].start()
    for p in range(PARTS):
        for i in range(len(peers)):
            r_copy(ro, rf_s, rf_r, p, i).wait_send()
    for store in stores:
        store.wait()


def solution(mesh):
    samp_count = mesh.shape["samp"]
    feat_count = mesh.shape["feat"]
    ring = math.isqrt(samp_count)
    chips = feat_count // 2

    def local_solve(x_loc, w_loc, y_loc, eta_loc):
        rows, width = x_loc.shape
        samples = rows * samp_count
        ridge = RIDGE_SCALE * (width * feat_count) / samples
        group = width // 2 // ring
        chunk = group // ring
        piece = rows // feat_count
        npeer = feat_count - 1
        dma = pltpu.SemaphoreType.DMA
        v = pltpu.VMEM
        scratch = [
            v((rows, width), BF16),
            v((width, rows), BF16),
            v((width, PARTS * LANES), F32),
            v((PARTS, 2, chunk, LANES), F32),
            v((PARTS, piece, LANES), F32),
            v((width // LANES, LANES), F32),
            v((LANES, LANES), F32),
            v((2, chunk, LANES), F32),
            v((PARTS, width, LANES), F32),
            v((PARTS, 2, ring - 1, group, LANES), F32),
            v((PARTS, 2, group, LANES), F32),
            v((PARTS, 2, ring - 1, chunk, LANES), F32),
            v((PARTS, width, LANES), BF16),
            v((PARTS, rows, LANES), BF16),
            v((PARTS, npeer, piece, LANES), BF16),
            v((PARTS, rows, LANES), BF16),
            v((PARTS, width, LANES), F32),
            v((PARTS, rows, LANES), F32),
            dma((3 + PARTS,)), dma((2 * PARTS,)),
        ]
        step1 = (PARTS, 2, ring - 1)
        step2 = (PARTS, 2, ring, ring - 1)
        scratch += [dma(step1)] * 6 + [dma(step2)] * 2 + [dma((PARTS, npeer))] * 4
        scratch += [dma(step1)] * 2 + [dma(step2)] * 2 + [dma((PARTS, npeer))] * 2
        return pl.pallas_call(
            functools.partial(ridge_kernel, ring, chips, samples, ridge),
            out_shape=[jax.ShapeDtypeStruct(w_loc.shape, F32), jax.ShapeDtypeStruct(y_loc.shape, F32)],
            in_specs=[pl.BlockSpec(memory_space=pl.ANY)] * 4,
            out_specs=[pl.BlockSpec(memory_space=pl.ANY)] * 2,
            scratch_shapes=scratch,
            compiler_params=pltpu.CompilerParams(
                collective_id=0, has_side_effects=True, vmem_limit_bytes=60 * 1024 * 1024),
        )(x_loc, w_loc, y_loc, eta_loc.reshape(width // LANES, LANES))

    return jax.shard_map(
        local_solve,
        mesh=mesh,
        in_specs=(P(("prob", "samp"), "feat"), P(("prob", "feat"), None), P(("prob", "samp"), None), P(("prob", "feat"))),
        out_specs=(P(("prob", "feat"), None), P(("prob", "samp"), None)),
        check_vma=False,
    )
```

time: 716 us -> 169 us (0.24)
  waiting for transfers between devices: 647 us -> 0 us
  Pallas kernels: 0 us -> 164 us
  matrix products: 30.5 us -> 0 us
  other arithmetic: 14.6 us -> 0 us
  between operations: 13.9 us -> 0.65 us
    psum x9 -> x0, waiting for transfers between devices: 647 us -> none  [the longest x4 355 us: local_solve(): gradient = lax.psum(part_grad, 'samp') / samples]
    pallas_call x0 -> x1, Pallas kernels: none -> 164 us  [local_solve(): pl.pallas_call(functools.partial(ridge_kernel, ring, chips, samples, ridg...]
    dot_general x9 -> x0, matrix products: 30.5 us -> none  [the longest x4 17.1 us: local_solve(): jnp.dot(x_loc, delta.astype(jnp.bfloat16), preferred_element_type=jnp.flo...]
    add x2 -> x0, other arithmetic: 10.3 us -> none  [local_solve(): weights = weights + COMBINE_WEIGHT * delta]
  transfers between devices with their start and end apart: 9 -> 0, of which waited for: 9 -> 0; matrix products, arithmetic and copies ran while one was open for 2% -> 0% of each run, Pallas kernels for 0% -> 0%
where the time goes in v1:
time: 169 us
  Pallas kernels  164 us (97%)
  local copies, waits for them, and re-layouts  3.9 us (2%)
    pallas_call x1, Pallas kernels, local_solve(): pl.pallas_call(functools.partial(ridge_kernel, ring, chips, samples, ridg...  164 us
    unnamed x4, local copies, waits for them, and re-layouts  3.9 us

profile of v1, /device:TPU:1, one launch (start us, length us, event | category | flops | bytes accessed | tf_op | source)
XLA Modules:
  0.0 168.9 jit_solution(6539875147637537816)
XLA Ops:
  0.6 164.3 %shard_map.59 = (f32[2048,256]{1,0:T(8,128)}, f32[512,256]{1,0:T(8,128)}) custom-call(bf16[512,2048]{1,0:T(8,128)(2,1)} %x_hbm.1, f32[2048,256]{1,0:T(8,128)} %w_hbm.1, f32[512,256]{1,0:T(8,128)} %y_hbm.1, f32[16,128]{1,0:T(8,128)} %bitcast.1), custom_call_target="tpu_custom_call" | custom-call | tf_op jit(solution)/shard_map/pallas_call | solution.py:319
  165.0 0.0 copy-start
  165.0 3.1 %copy.8 = f32[2048,256]{1,0:T(8,128)} copy(f32[2048,256]{1,0:T(8,128)} %get-tuple-element.4) | data formatting | bytes 4194304
  168.1 0.0 copy-done
  168.1 0.8 copy.9
Async XLA Ops:
  165.0 3.1 %copy-start = (f32[512,256]{1,0:T(8,128)S(1)}, f32[512,256]{1,0:T(8,128)}, u32[]{:S(2)}) copy-start(f32[512,256]{1,0:T(8,128)} %get-tuple-element.5) | copy-start | bytes 1572868

commit v2 on v1

--- a/solution.py
+++ b/solution.py
@@ -19,7 +19,7 @@
 
 
 def ridge_kernel(ring, chips, samples, ridge, x_hbm, w_hbm, y_hbm, eta_hbm, wo_hbm, ro_hbm,
-                 x, xt, w_in, w, r, eta_in, eta_t, eta, g, rs1, s1, rs2, dw, u, ur, rb, wo, ro,
+                 x, xt, w_in, w, r, eta_in, eta_t, eta, g, rs1, near, far, s1, rs2, dw, u, ur, rb, wo, ro,
                  load_sem, store_sem,
                  rs1_s, rs1_r, rs2_s, rs2_r, ag1_s, ag1_r, ag2_s, ag2_r,
                  u_s, u_r, rg_s, rg_r, wg1_s, wg1_r, wg2_s, wg2_r, rf_s, rf_r):
@@ -38,7 +38,11 @@
     seconds = (zs, ys)
     neighbour = [[cz * ring + c for c in ys], [c * ring + cy for c in zs]]
     far_first = sorted(range(1, ring), key=lambda d: -min(d, ring - d))
-    peers = [(dx, dc) for dx in far_first + [0] for dc in (0, 1) if dx or dc]
+    near_first = far_first[::-1]
+    sides = (1, ring - 1)
+    hg = group // 2
+    across = sorted(range(1, chips), key=lambda d: -min(d, chips - d))
+    peers = [(dx, dc) for dx in across + [0] for dc in (0, 1) if dx or dc]
 
     xs = [cx] + [lax.rem(cx + d, chips) for d in range(1, chips)]
     cores = [core, 1 - core]
@@ -65,9 +69,14 @@
     def chunk_at(h, e):
         return pl.ds(own_chunks[h][e], chunk)
 
-    def rs1_copy(p, h, d):
-        return remote(g.at[p, group_at(h, d)], rs1.at[p, h, d - 1],
-                      rs1_s.at[p, h, d - 1], rs1_r.at[p, h, d - 1], along(h, d))
+    def rs1_copy(p, h, kind, k):
+        if kind == 0:
+            row, dst = group_rows[h][2] + k * hg, rs1.at[p, h, k]
+        elif kind == 1:
+            row, dst = group_rows[h][sides[k]] + (1 - k) * hg, near.at[p, h, pl.ds((1 - k) * hg, hg)]
+        else:
+            row, dst = group_rows[h][sides[k]] + k * hg, far.at[p, h, pl.ds(k * hg, hg)]
+        return remote(g.at[p, pl.ds(row, hg)], dst, rs1_s.at[p, h, kind, k], rs1_r.at[p, h, kind, k], along(h, sides[k]))
 
     def rs2_copy(p, h, d):
         return remote(s1.at[p, h, part_at(h, d)], rs2.at[p, h, d - 1],
@@ -77,9 +86,14 @@
         at = chunk_at(h, 0)
         return remote(buf.at[p, at], buf.at[p, at], ss.at[p, h, d - 1], rr.at[p, h, d - 1], along(1 - h, d))
 
-    def gather2(buf, ss, rr, p, h, e, d):
+    def gather2(buf, ss, rr, p, h, e, k):
         at = chunk_at(h, (ring - e) % ring)
-        return remote(buf.at[p, at], buf.at[p, at], ss.at[p, h, e, d - 1], rr.at[p, h, e, d - 1], along(h, d))
+        return remote(buf.at[p, at], buf.at[p, at], ss.at[p, h, 0, e, k], rr.at[p, h, 0, e, k], along(h, sides[k]))
+
+    def gather3(buf, ss, rr, p, h, e, k):
+        row = group_rows[h][ring - sides[k]] + chunk_rows[h][(ring - e) % ring] + k * (chunk // 2)
+        at = pl.ds(row, chunk // 2)
+        return remote(buf.at[p, at], buf.at[p, at], ss.at[p, h, 1, e, k], rr.at[p, h, 1, e, k], along(h, sides[k]))
 
     def u_copy(p, i):
         return remote(u.at[p, pl.ds(piece_rows[i], piece)], ur.at[p, i], u_s.at[p, i], u_r.at[p, i], {"feat": feats[i]})
@@ -113,26 +127,42 @@
     def start_g(p):
         for i in range(len(peers)):
             r_copy(rb, rg_s, rg_r, p, i).wait_recv()
-        for d in far_first + [0]:
+        for d in (2, 1, ring - 1, 0):
             for h in (0, 1):
                 at = group_at(h, d)
                 g[p, at] = jnp.dot(xt[at], rb[p], preferred_element_type=F32)
-                if d:
-                    rs1_copy(p, h, d).start()
+                for k in (0, 1):
+                    if d == 2:
+                        rs1_copy(p, h, 0, k).start()
+                    elif d == sides[k]:
+                        rs1_copy(p, h, 1, k).start()
         for i in range(len(peers)):
             r_copy(rb, rg_s, rg_r, p, i).wait_send()
 
+    def pass_g(p):
+        for h in (0, 1):
+            for k in (0, 1):
+                rs1_copy(p, h, 0, k).wait_recv()
+                at = pl.ds(group_rows[h][sides[k]] + k * hg, hg)
+                g[p, at] = g[p, at] + rs1[p, h, k]
+                rs1_copy(p, h, 2, k).start()
+
     def mid_g(p):
         for h in (0, 1):
-            for d in range(1, ring):
-                rs1_copy(p, h, d).wait_recv()
+            for k in (0, 1):
+                rs1_copy(p, h, 1, k).wait_recv()
+                rs1_copy(p, h, 2, k).wait_recv()
             for e in far_first + [0]:
-                total = g[p, chunk_at(h, e)]
-                for d in range(1, ring):
-                    total = total + rs1[p, h, d - 1, part_at(h, e)]
-                s1[p, h, part_at(h, e)] = total
+                at = part_at(h, e)
+                s1[p, h, at] = g[p, chunk_at(h, e)] + near[p, h, at] + far[p, h, at]
                 if e:
                     rs2_copy(p, h, e).start()
+
+    def first_gather(buf, s1_, r1_, s2_, r2_, p, h):
+        for d in near_first:
+            gather1(buf, s1_, r1_, p, h, d).start()
+        for k in (0, 1):
+            gather2(buf, s2_, r2_, p, h, 0, k).start()
 
     def end_g(p, last):
         for h in (0, 1):
@@ -144,37 +174,43 @@
             delta = eta[h] * (total / samples - ridge * w[p, h])
             at = chunk_at(h, 0)
             dw[p, at] = delta.astype(BF16)
-            for d in far_first:
-                gather1(dw, ag1_s, ag1_r, p, h, d).start()
-            for d in far_first:
-                gather2(dw, ag2_s, ag2_r, p, h, 0, d).start()
+            first_gather(*ag, p, h)
             new = w[p, h] + COMBINE_WEIGHT * delta
             w[p, h] = new
             if last:
                 wo[p, at] = new
 
-    def relay(buf, s1_, r1_, s2_, r2_, p):
-        for e in range(1, ring):
+    def relay1(buf, s1_, r1_, s2_, r2_, p):
+        for e in near_first:
             for h in (0, 1):
                 gather1(buf, s1_, r1_, p, h, e).wait_recv()
-                for d in far_first:
-                    gather2(buf, s2_, r2_, p, h, e, d).start()
+                for k in (0, 1):
+                    gather2(buf, s2_, r2_, p, h, e, k).start()
+
+    def relay2(buf, s1_, r1_, s2_, r2_, p):
+        for e in [0] + near_first:
+            for h in (0, 1):
+                for k in (0, 1):
+                    gather2(buf, s2_, r2_, p, h, e, k).wait_recv()
+                    gather3(buf, s2_, r2_, p, h, e, k).start()
 
     def gathered(buf, s1_, r1_, s2_, r2_, p):
-        for h in (0, 1):
-            for e in range(ring):
-                for d in range(1, ring):
-                    gather2(buf, s2_, r2_, p, h, e, d).wait_recv()
-        for h in (0, 1):
+        each = [(h, e, k) for e in [0] + near_first for h in (0, 1) for k in (0, 1)]
+        for h, e, k in each:
+            gather3(buf, s2_, r2_, p, h, e, k).wait_recv()
+        for h in (0, 1):
+            for d in near_first:
+                gather1(buf, s1_, r1_, p, h, d).wait_send()
+        for h, e, k in each:
+            gather2(buf, s2_, r2_, p, h, e, k).wait_send()
+            gather3(buf, s2_, r2_, p, h, e, k).wait_send()
+
+    def sent_g(p):
+        for h in (0, 1):
+            for kind in range(3):
+                for k in (0, 1):
+                    rs1_copy(p, h, kind, k).wait_send()
             for d in range(1, ring):
-                gather1(buf, s1_, r1_, p, h, d).wait_send()
-                for e in range(ring):
-                    gather2(buf, s2_, r2_, p, h, e, d).wait_send()
-
-    def sent_g(p):
-        for h in (0, 1):
-            for d in range(1, ring):
-                rs1_copy(p, h, d).wait_send()
                 rs2_copy(p, h, d).wait_send()
 
     ag = (dw, ag1_s, ag1_r, ag2_s, ag2_r)
@@ -223,25 +259,26 @@
         for p in range(PARTS):
             start_g(p)
         for p in range(PARTS):
+            pass_g(p)
+        for p in range(PARTS):
             mid_g(p)
         for p in range(PARTS):
             end_g(p, last)
         for p in range(PARTS):
-            relay(*ag, p)
+            relay1(*ag, p)
+        for p in range(PARTS):
+            relay2(*ag, p)
         if last:
             for p in range(PARTS):
                 for h in (0, 1):
-                    for d in far_first:
-                        gather1(*wg[:3], p, h, d).start()
-                    for d in far_first:
-                        gather2(wo, wg2_s, wg2_r, p, h, 0, d).start()
+                    first_gather(*wg, p, h)
         for p in range(PARTS):
             sent_g(p)
             gathered(*ag, p)
             start_u(p)
         if last:
             for p in range(PARTS):
-                relay(*wg, p)
+                relay1(*wg, p)
         for p in range(PARTS):
             r[p] = r[p] - COMBINE_WEIGHT * sum_u(p)
             if last:
@@ -250,6 +287,9 @@
                     r_copy(ro, rf_s, rf_r, p, i).start()
             else:
                 send_r(p)
+        if last:
+            for p in range(PARTS):
+                relay2(*wg, p)
 
     def body(i, carry):
         sweep(False)
@@ -301,7 +341,9 @@
             v((LANES, LANES), F32),
             v((2, chunk, LANES), F32),
             v((PARTS, width, LANES), F32),
-            v((PARTS, 2, ring - 1, group, LANES), F32),
+            v((PARTS, 2, 2, group // 2, LANES), F32),
+            v((PARTS, 2, group, LANES), F32),
+            v((PARTS, 2, group, LANES), F32),
             v((PARTS, 2, group, LANES), F32),
             v((PARTS, 2, ring - 1, chunk, LANES), F32),
             v((PARTS, width, LANES), BF16),
@@ -313,8 +355,8 @@
             dma((3 + PARTS,)), dma((2 * PARTS,)),
         ]
         step1 = (PARTS, 2, ring - 1)
-        step2 = (PARTS, 2, ring, ring - 1)
-        scratch += [dma(step1)] * 6 + [dma(step2)] * 2 + [dma((PARTS, npeer))] * 4
+        step2 = (PARTS, 2, 2, ring, 2)
+        scratch += [dma((PARTS, 2, 3, 2))] * 2 + [dma(step1)] * 4 + [dma(step2)] * 2 + [dma((PARTS, npeer))] * 4
         scratch += [dma(step1)] * 2 + [dma(step2)] * 2 + [dma((PARTS, npeer))] * 2
         return pl.pallas_call(
             functools.partial(ridge_kernel, ring, chips, samples, ridge),

time: 169 us -> 169 us (level)
  no operation moved by 1% of the time
where the time goes in v2:
time: 169 us
  Pallas kernels  164 us (97%)
  local copies, waits for them, and re-layouts  3.9 us (2%)
    pallas_call x1, Pallas kernels, local_solve(): pl.pallas_call(functools.partial(ridge_kernel, ring, chips, samples, ridg...  164 us
    unnamed x4, local copies, waits for them, and re-layouts  3.9 us

profile of v2, /device:TPU:1, one launch (start us, length us, event | category | flops | bytes accessed | tf_op | source)
XLA Modules:
  0.0 168.8 jit_solution(1475620210838632344)
XLA Ops:
  0.6 164.2 %shard_map.59 = (f32[2048,256]{1,0:T(8,128)}, f32[512,256]{1,0:T(8,128)}) custom-call(bf16[512,2048]{1,0:T(8,128)(2,1)} %x_hbm.1, f32[2048,256]{1,0:T(8,128)} %w_hbm.1, f32[512,256]{1,0:T(8,128)} %y_hbm.1, f32[16,128]{1,0:T(8,128)} %bitcast.1), custom_call_target="tpu_custom_call" | custom-call | tf_op jit(solution)/shard_map/pallas_call | solution.py:361
  164.9 0.0 copy-start
  164.9 3.1 %copy.8 = f32[2048,256]{1,0:T(8,128)} copy(f32[2048,256]{1,0:T(8,128)} %get-tuple-element.4) | data formatting | bytes 4194304
  168.0 0.0 copy-done
  168.0 0.8 copy.9
Async XLA Ops:
  164.9 3.1 %copy-start = (f32[512,256]{1,0:T(8,128)S(1)}, f32[512,256]{1,0:T(8,128)}, u32[]{:S(2)}) copy-start(f32[512,256]{1,0:T(8,128)} %get-tuple-element.5) | copy-start | bytes 1572868

commit v3 on v2

v3 whole, which is shorter than its diff:
```python
import functools
import math

import jax
import jax.numpy as jnp
from jax import lax
from jax.experimental import pallas as pl
from jax.experimental.pallas import tpu as pltpu
from jax.sharding import PartitionSpec as P

SWEEPS = 4
COMBINE_WEIGHT = 0.8
RIDGE_SCALE = 0.1
PARTS = 2
LANES = 128
QUARTERS = 4
UNITS = ((0, 1), (2, 3))
MESH = pl.DeviceIdType.MESH
F32 = jnp.float32
BF16 = jnp.bfloat16


def ridge_kernel(ring, chips, samples, ridge, x_hbm, w_hbm, y_hbm, eta_hbm, wo, ro,
                 x, xt, w_in, w, r, eta_in, eta_t, eta, g, rs1, near, far, s1, rs2, dw, u, ur, rb,
                 load_sem, rl_r, nf_r, rs2_r, gs_s, ag1_r, ag2_r, ag3_r, ag_s,
                 u_s, u_r, rg_s, rg_r, wg1_r, wg2_r, wg3_r, wg_s, rf_s, rf_r):
    samp = lax.axis_index("samp")
    feat = lax.axis_index("feat")
    rows, width = x.shape
    quarter = width // QUARTERS
    group = quarter // ring
    chunk = group // ring
    hg = group // 2
    piece = rows // (2 * chips)
    cy, cz = lax.rem(samp, ring), lax.div(samp, ring)
    cx, core = lax.div(feat, 2), lax.rem(feat, 2)
    ys = [cy] + [lax.rem(cy + d, ring) for d in range(1, ring)]
    zs = [cz] + [lax.rem(cz + d, ring) for d in range(1, ring)]
    neighbour = [[cz * ring + c for c in ys], [c * ring + cy for c in zs]]
    far_first = sorted(range(1, ring), key=lambda d: -min(d, ring - d))
    near_first = far_first[::-1]
    sides = (1, ring - 1)
    across = sorted(range(1, chips), key=lambda d: -min(d, chips - d))
    peers = [(dx, dc) for dx in across + [0] for dc in (0, 1) if dx or dc]
    xs = [cx] + [lax.rem(cx + d, chips) for d in range(1, chips)]
    cores = [core, 1 - core]
    feats = [xs[dx] * 2 + cores[dc] for dx, dc in peers]
    firsts = [(ys, zs)[h % 2] for h in range(QUARTERS)]
    seconds = [(zs, ys)[h % 2] for h in range(QUARTERS)]
    group_rows = [[h * quarter + c * group for c in firsts[h]] for h in range(QUARTERS)]
    chunk_rows = [[c * chunk for c in seconds[h]] for h in range(QUARTERS)]
    own_chunks = [[group_rows[h][0] + c for c in chunk_rows[h]] for h in range(QUARTERS)]
    piece_rows = [f * piece for f in feats]
    mine = pl.ds(feat * piece, piece)
    everything = tuple(range(QUARTERS))

    def along(axis, d):
        return {"samp": neighbour[axis % 2][d]}

    def remote(src, dst, send, recv, device):
        return pltpu.make_async_remote_copy(
            src_ref=src, dst_ref=dst, send_sem=send, recv_sem=recv, device_id=device, device_id_type=MESH)

    def drain(ref, sem):
        pltpu.make_async_copy(ref, ref, sem).wait()

    def group_at(h, d):
        return pl.ds(group_rows[h][d], group)

    def part_at(h, e):
        return pl.ds(chunk_rows[h][e], chunk)

    def chunk_at(h, e):
        return pl.ds(own_chunks[h][e], chunk)

    def columns(p):
        return pl.ds(p * LANES, LANES)

    def rs1_copy(p, h, kind, k):
        if kind == 0:
            row, dst, sem = group_rows[h][2] + k * hg, rs1.at[p, h, k], rl_r.at[p, h, k]
        elif kind == 1:
            row, dst, sem = group_rows[h][sides[k]] + (1 - k) * hg, near.at[p, h, pl.ds((1 - k) * hg, hg)], nf_r.at[p, h]
        else:
            row, dst, sem = group_rows[h][sides[k]] + k * hg, far.at[p, h, pl.ds(k * hg, hg)], nf_r.at[p, h]
        return remote(g.at[p, pl.ds(row, hg)], dst, gs_s.at[p], sem, along(h, sides[k]))

    def rs2_copy(p, h, d):
        return remote(s1.at[p, h, part_at(h, d)], rs2.at[p, h, d - 1], gs_s.at[p], rs2_r.at[p, h], along(h + 1, d))

    def u_copy(p, i):
        return remote(u.at[p, pl.ds(piece_rows[i], piece)], ur.at[p, i], u_s.at[p], u_r.at[p], {"feat": feats[i]})

    def r_copy(ref, ss, rr, p, i):
        return remote(ref, ref, ss.at[p], rr.at[p], {"feat": feats[i]})

    class Gather:
        def __init__(self, view, r1, r2, r3, s):
            self.view, self.r1, self.r2, self.r3, self.s = view, r1, r2, r3, s

        def first(self, p, h):
            ref = self.view(p, chunk_at(h, 0))
            for d in near_first:
                remote(ref, ref, self.s.at[p], self.r1.at[p, h], along(h + 1, d)).start()

        def second(self, p, h):
            drain(self.view(p, pl.ds(0, (ring - 1) * chunk)), self.r1.at[p, h])
            ref = self.view(p, group_at(h, 0))
            for k in (0, 1):
                remote(ref, ref, self.s.at[p], self.r2.at[p, h, k], along(h, sides[k])).start()

        def third(self, p, h):
            for k in (0, 1):
                drain(self.view(p, pl.ds(0, group)), self.r2.at[p, h, k])
                ref = self.view(p, pl.ds(group_rows[h][ring - sides[k]] + k * hg, hg))
                remote(ref, ref, self.s.at[p], self.r3.at[p, h], along(h, sides[k])).start()

        def last(self, p, h):
            drain(self.view(p, pl.ds(0, group)), self.r3.at[p, h])

        def sent(self, p):
            drain(self.view(p, pl.ds(0, QUARTERS * ((ring - 1) * chunk + 3 * group))), self.s.at[p])

    ag = Gather(lambda p, at: dw.at[p, at], ag1_r, ag2_r, ag3_r, ag_s)
    wg = Gather(lambda p, at: wo.at[at, columns(p)], wg1_r, wg2_r, wg3_r, wg_s)

    def start_u(p):
        step = max(rows // 2, piece)
        for k in range(rows // step):
            at = pl.ds(k * step, step)
            u[p, at] = jnp.dot(x[at], dw[p], preferred_element_type=F32).astype(BF16)
        for i in range(len(peers)):
            u_copy(p, i).start()

    def sum_u(p):
        total = u[p, mine].astype(F32)
        drain(ur.at[p], u_r.at[p])
        for i in range(len(peers)):
            total = total + ur[p, i].astype(F32)
        drain(ur.at[p], u_s.at[p])
        return total

    def send_r(p):
        rb[p, mine] = r[p].astype(BF16)
        for i in range(len(peers)):
            r_copy(rb.at[p, mine], rg_s, rg_r, p, i).start()

    def start_g(p, hs):
        if hs == UNITS[0]:
            drain(ur.at[p], rg_r.at[p])
        for ds in ((2,), (1, ring - 1), (0,)):
            for d in ds:
                for h in hs:
                    at = group_at(h, d)
                    g[p, at] = jnp.dot(xt[at], rb[p], preferred_element_type=F32)
            for h in hs:
                for k in (0, 1):
                    if ds[0] == 2:
                        rs1_copy(p, h, 0, k).start()
                    elif ds[0]:
                        rs1_copy(p, h, 1, k).start()

    def pass_g(p, hs):
        for h in hs:
            for k in (0, 1):
                rs1_copy(p, h, 0, k).wait_recv()
                at = pl.ds(group_rows[h][sides[k]] + k * hg, hg)
                g[p, at] = g[p, at] + rs1[p, h, k]
                rs1_copy(p, h, 2, k).start()

    def mid_g(p, hs):
        for h in hs:
            drain(g.at[p, pl.ds(0, 2 * group)], nf_r.at[p, h])
            for e in far_first + [0]:
                at = part_at(h, e)
                s1[p, h, at] = g[p, chunk_at(h, e)] + near[p, h, at] + far[p, h, at]
                if e:
                    rs2_copy(p, h, e).start()

    def end_g(p, hs, last):
        for h in hs:
            drain(g.at[p, pl.ds(0, (ring - 1) * chunk)], rs2_r.at[p, h])
            total = s1[p, h, part_at(h, 0)]
            for d in range(1, ring):
                total = total + rs2[p, h, d - 1]
            delta = eta[h] * (total / samples - ridge * w[p, h])
            at = chunk_at(h, 0)
            dw[p, at] = delta.astype(BF16)
            ag.first(p, h)
            new = w[p, h] + COMBINE_WEIGHT * delta
            w[p, h] = new
            if last:
                wo[at, p * LANES:(p + 1) * LANES] = new

    loads = [pltpu.make_async_copy(w_hbm, w_in, load_sem.at[0]),
             pltpu.make_async_copy(x_hbm, x, load_sem.at[1]),
             pltpu.make_async_copy(eta_hbm, eta_in, load_sem.at[2])]
    loads += [pltpu.make_async_copy(y_hbm.at[mine, columns(p)], r.at[p], load_sem.at[3 + p]) for p in range(PARTS)]
    for load in loads:
        load.start()
    barrier = pltpu.get_barrier_semaphore()
    for d in range(1, ring):
        for axis in (0, 1):
            pl.semaphore_signal(barrier, inc=1, device_id=along(axis, d), device_id_type=MESH)
    for i in range(len(peers)):
        pl.semaphore_signal(barrier, inc=1, device_id={"feat": feats[i]}, device_id_type=MESH)
    loads[0].wait()
    for p in range(PARTS):
        dw[p] = w_in[:, p * LANES:(p + 1) * LANES].astype(BF16)
        for h in everything:
            w[p, h] = w_in[chunk_at(h, 0), p * LANES:(p + 1) * LANES]
    loads[1].wait()
    pl.semaphore_wait(barrier, 2 * (ring - 1) + len(peers))

    for p in range(PARTS):
        start_u(p)
    tile = min(width, 256)
    for k in range(width // tile):
        xt[k * tile:(k + 1) * tile] = x[:, k * tile:(k + 1) * tile].T
    loads[2].wait()
    for h in everything:
        pos = own_chunks[h][0]
        line = eta_in[pl.ds(lax.div(pos, LANES), 1), :]
        eta_t[...] = jnp.broadcast_to(line, (LANES, LANES)).T
        eta[h] = eta_t[pl.ds(lax.rem(pos, LANES), chunk), :]
    for p in range(PARTS):
        loads[3 + p].wait()
        r[p] = r[p] - sum_u(p)
        send_r(p)

    def sweep(last):
        both = [(p, hs) for p in range(PARTS) for hs in UNITS]
        for p, hs in both:
            start_g(p, hs)
        for p in range(PARTS):
            drain(ur.at[p], rg_s.at[p])
        for p, hs in both:
            pass_g(p, hs)
        for p, hs in both:
            mid_g(p, hs)
        for p, hs in both:
            end_g(p, hs, last)
        for p, hs in both:
            for h in hs:
                ag.second(p, h)
        for p, hs in both:
            for h in hs:
                ag.third(p, h)
        if last:
            for p in range(PARTS):
                for h in everything:
                    wg.first(p, h)
        for p in range(PARTS):
            drain(g.at[p, pl.ds(0, QUARTERS * (3 * group + (ring - 1) * chunk))], gs_s.at[p])
            for h in everything:
                ag.last(p, h)
            ag.sent(p)
            start_u(p)
        if last:
            for p in range(PARTS):
                for h in everything:
                    wg.second(p, h)
        for p in range(PARTS):
            r[p] = r[p] - COMBINE_WEIGHT * sum_u(p)
            if last:
                ro[mine, p * LANES:(p + 1) * LANES] = r[p]
                for i in range(len(peers)):
                    r_copy(ro.at[mine, columns(p)], rf_s, rf_r, p, i).start()
            else:
                send_r(p)
        if last:
            for p in range(PARTS):
                for h in everything:
                    wg.third(p, h)

    def body(i, carry):
        sweep(False)
        return carry

    lax.fori_loop(0, SWEEPS - 1, body, 0)
    sweep(True)
    for p in range(PARTS):
        final = ro.at[pl.ds(0, len(peers) * piece), columns(p)]
        drain(final, rf_r.at[p])
        drain(final, rf_s.at[p])
    for p in range(PARTS):
        for h in everything:
            wg.last(p, h)
        wg.sent(p)


def solution(mesh):
    samp_count = mesh.shape["samp"]
    feat_count = mesh.shape["feat"]
    ring = math.isqrt(samp_count)
    chips = feat_count // 2

    def local_solve(x_loc, w_loc, y_loc, eta_loc):
        rows, width = x_loc.shape
        samples = rows * samp_count
        ridge = RIDGE_SCALE * (width * feat_count) / samples
        group = width // QUARTERS // ring
        chunk = group // ring
        piece = rows // feat_count
        npeer = feat_count - 1
        dma = pltpu.SemaphoreType.DMA
        v = pltpu.VMEM
        each = (PARTS, QUARTERS)
        scratch = [
            v((rows, width), BF16),
            v((width, rows), BF16),
            v((width, PARTS * LANES), F32),
            v(each + (chunk, LANES), F32),
            v((PARTS, piece, LANES), F32),
            v((width // LANES, LANES), F32),
            v((LANES, LANES), F32),
            v((QUARTERS, chunk, LANES), F32),
            v((PARTS, width, LANES), F32),
            v(each + (2, group // 2, LANES), F32),
            v(each + (group, LANES), F32),
            v(each + (group, LANES), F32),
            v(each + (group, LANES), F32),
            v(each + (ring - 1, chunk, LANES), F32),
            v((PARTS, width, LANES), BF16),
            v((PARTS, rows, LANES), BF16),
            v((PARTS, npeer, piece, LANES), BF16),
            v((PARTS, rows, LANES), BF16),
            dma((3 + PARTS,)),
            dma(each + (2,)), dma(each), dma(each), dma((PARTS,)),
            dma(each), dma(each + (2,)), dma(each), dma((PARTS,)),
            dma((PARTS,)), dma((PARTS,)), dma((PARTS,)), dma((PARTS,)),
            dma(each), dma(each + (2,)), dma(each), dma((PARTS,)),
            dma((PARTS,)), dma((PARTS,)),
        ]
        return pl.pallas_call(
            functools.partial(ridge_kernel, ring, chips, samples, ridge),
            out_shape=[pltpu.VMEM(w_loc.shape, F32), pltpu.VMEM(y_loc.shape, F32)],
            in_specs=[pl.BlockSpec(memory_space=pltpu.HBM)] * 4,
            out_specs=[pl.BlockSpec(memory_space=pltpu.VMEM)] * 2,
            scratch_shapes=scratch,
            compiler_params=pltpu.CompilerParams(
                collective_id=0, has_side_effects=True, vmem_limit_bytes=56 * 1024 * 1024),
        )(x_loc, w_loc, y_loc, eta_loc.reshape(width // LANES, LANES))

    return jax.shard_map(
        local_solve,
        mesh=mesh,
        in_specs=(P(("prob", "samp"), "feat"), P(("prob", "feat"), None), P(("prob", "samp"), None), P(("prob", "feat"))),
        out_specs=(P(("prob", "feat"), None), P(("prob", "samp"), None)),
        check_vma=False,
    )
```

time: 169 us -> 158 us (0.935)
  Pallas kernels: 164 us -> 155 us
  local copies, waits for them, and re-layouts: 3.9 us -> 2.11 us
    pallas_call x1, Pallas kernels: 164 us -> 155 us  [local_solve(): pl.pallas_call(functools.partial(ridge_kernel, ring, chips, samples, ridg...]
    unnamed x4 -> x2, local copies, waits for them, and re-layouts: 3.9 us -> 2.11 us
where the time goes in v3:
time: 158 us
  Pallas kernels  155 us (98%)
  local copies, waits for them, and re-layouts  2.11 us (1%)
    pallas_call x1, Pallas kernels, local_solve(): pl.pallas_call(functools.partial(ridge_kernel, ring, chips, samples, ridg...  155 us

profile of v3, /device:TPU:1, one launch (start us, length us, event | category | flops | bytes accessed | tf_op | source)
XLA Modules:
  0.0 157.9 jit_solution(16044346372391021823)
XLA Ops:
  0.6 155.1 %shard_map.59 = (f32[2048,256]{1,0:T(8,128)S(1)}, f32[512,256]{1,0:T(8,128)S(1)}) custom-call(bf16[512,2048]{1,0:T(8,128)(2,1)} %x_hbm.1, f32[2048,256]{1,0:T(8,128)} %w_hbm.1, f32[512,256]{1,0:T(8,128)} %y_hbm.1, f32[16,128]{1,0:T(8,128)} %bitcast.1), custom_call_target="tpu_custom_call" | custom-call | tf_op jit(solution)/shard_map/pallas_call | solution.py:335
  155.8 1.3 copy.8
  157.1 0.8 copy.9

commit v4 on v3

--- a/solution.py
+++ b/solution.py
@@ -22,7 +22,7 @@
 
 def ridge_kernel(ring, chips, samples, ridge, x_hbm, w_hbm, y_hbm, eta_hbm, wo, ro,
                  x, xt, w_in, w, r, eta_in, eta_t, eta, g, rs1, near, far, s1, rs2, dw, u, ur, rb,
-                 load_sem, rl_r, nf_r, rs2_r, gs_s, ag1_r, ag2_r, ag3_r, ag_s,
+                 load_sem, rl_r, nf_r, rs2_r, gs_s, ag1_r, ag3_r, ag_s,
                  u_s, u_r, rg_s, rg_r, wg1_r, wg2_r, wg3_r, wg_s, rf_s, rf_r):
     samp = lax.axis_index("samp")
     feat = lax.axis_index("feat")
@@ -106,8 +106,12 @@
         def second(self, p, h):
             drain(self.view(p, pl.ds(0, (ring - 1) * chunk)), self.r1.at[p, h])
             ref = self.view(p, group_at(h, 0))
-            for k in (0, 1):
-                remote(ref, ref, self.s.at[p], self.r2.at[p, h, k], along(h, sides[k])).start()
+            if self.r2 is None:
+                for d in far_first:
+                    remote(ref, ref, self.s.at[p], self.r3.at[p, h], along(h, d)).start()
+            else:
+                for k in (0, 1):
+                    remote(ref, ref, self.s.at[p], self.r2.at[p, h, k], along(h, sides[k])).start()
 
         def third(self, p, h):
             for k in (0, 1):
@@ -116,12 +120,12 @@
                 remote(ref, ref, self.s.at[p], self.r3.at[p, h], along(h, sides[k])).start()
 
         def last(self, p, h):
-            drain(self.view(p, pl.ds(0, group)), self.r3.at[p, h])
+            drain(self.view(p, pl.ds(0, group if self.r2 is not None else (ring - 1) * group)), self.r3.at[p, h])
 
         def sent(self, p):
             drain(self.view(p, pl.ds(0, QUARTERS * ((ring - 1) * chunk + 3 * group))), self.s.at[p])
 
-    ag = Gather(lambda p, at: dw.at[p, at], ag1_r, ag2_r, ag3_r, ag_s)
+    ag = Gather(lambda p, at: dw.at[p, at], ag1_r, None, ag3_r, ag_s)
     wg = Gather(lambda p, at: wo.at[at, columns(p)], wg1_r, wg2_r, wg3_r, wg_s)
 
     def start_u(p):
@@ -243,9 +247,6 @@
         for p, hs in both:
             for h in hs:
                 ag.second(p, h)
-        for p, hs in both:
-            for h in hs:
-                ag.third(p, h)
         if last:
             for p in range(PARTS):
                 for h in everything:
@@ -327,7 +328,7 @@
             v((PARTS, rows, LANES), BF16),
             dma((3 + PARTS,)),
             dma(each + (2,)), dma(each), dma(each), dma((PARTS,)),
-            dma(each), dma(each + (2,)), dma(each), dma((PARTS,)),
+            dma(each), dma(each), dma((PARTS,)),
             dma((PARTS,)), dma((PARTS,)), dma((PARTS,)), dma((PARTS,)),
             dma(each), dma(each + (2,)), dma(each), dma((PARTS,)),
             dma((PARTS,)), dma((PARTS,)),

time: 158 us -> 149 us (0.943)
  Pallas kernels: 155 us -> 146 us
    pallas_call x1, Pallas kernels: 155 us -> 146 us  [local_solve(): pl.pallas_call(functools.partial(ridge_kernel, ring, chips, samples, ridg...]
where the time goes in v4:
time: 149 us
  Pallas kernels  146 us (98%)
  local copies, waits for them, and re-layouts  2.11 us (1%)
    pallas_call x1, Pallas kernels, local_solve(): pl.pallas_call(functools.partial(ridge_kernel, ring, chips, samples, ridg...  146 us

profile of v4, /device:TPU:1, one launch (start us, length us, event | category | flops | bytes accessed | tf_op | source)
XLA Modules:
  0.0 148.9 jit_solution(13641251525499341644)
XLA Ops:
  0.6 146.2 %shard_map.59 = (f32[2048,256]{1,0:T(8,128)S(1)}, f32[512,256]{1,0:T(8,128)S(1)}) custom-call(bf16[512,2048]{1,0:T(8,128)(2,1)} %x_hbm.1, f32[2048,256]{1,0:T(8,128)} %w_hbm.1, f32[512,256]{1,0:T(8,128)} %y_hbm.1, f32[16,128]{1,0:T(8,128)} %bitcast.1), custom_call_target="tpu_custom_call" | custom-call | tf_op jit(solution)/shard_map/pallas_call | solution.py:336
  146.8 1.3 copy.8
  148.1 0.8 copy.9

commit v5 on v4

--- a/solution.py
+++ b/solution.py
@@ -21,8 +21,8 @@
 
 
 def ridge_kernel(ring, chips, samples, ridge, x_hbm, w_hbm, y_hbm, eta_hbm, wo, ro,
-                 x, xt, w_in, w, r, eta_in, eta_t, eta, g, rs1, near, far, s1, rs2, dw, u, ur, rb,
-                 load_sem, rl_r, nf_r, rs2_r, gs_s, ag1_r, ag3_r, ag_s,
+                 x, xt, w_in, w, r, eta_in, eta_t, eta, g, rs1, s1, rs2, dw, u, ur, rb,
+                 load_sem, rs1_r, rs2_r, gs_s, ag1_r, ag3_r, ag_s,
                  u_s, u_r, rg_s, rg_r, wg1_r, wg2_r, wg3_r, wg_s, rf_s, rf_r):
     samp = lax.axis_index("samp")
     feat = lax.axis_index("feat")
@@ -76,14 +76,8 @@
     def columns(p):
         return pl.ds(p * LANES, LANES)
 
-    def rs1_copy(p, h, kind, k):
-        if kind == 0:
-            row, dst, sem = group_rows[h][2] + k * hg, rs1.at[p, h, k], rl_r.at[p, h, k]
-        elif kind == 1:
-            row, dst, sem = group_rows[h][sides[k]] + (1 - k) * hg, near.at[p, h, pl.ds((1 - k) * hg, hg)], nf_r.at[p, h]
-        else:
-            row, dst, sem = group_rows[h][sides[k]] + k * hg, far.at[p, h, pl.ds(k * hg, hg)], nf_r.at[p, h]
-        return remote(g.at[p, pl.ds(row, hg)], dst, gs_s.at[p], sem, along(h, sides[k]))
+    def rs1_copy(p, h, d):
+        return remote(g.at[p, group_at(h, d)], rs1.at[p, h, d - 1], gs_s.at[p], rs1_r.at[p, h], along(h, d))
 
     def rs2_copy(p, h, d):
         return remote(s1.at[p, h, part_at(h, d)], rs2.at[p, h, d - 1], gs_s.at[p], rs2_r.at[p, h], along(h + 1, d))
@@ -157,27 +151,20 @@
                 for h in hs:
                     at = group_at(h, d)
                     g[p, at] = jnp.dot(xt[at], rb[p], preferred_element_type=F32)
-            for h in hs:
-                for k in (0, 1):
-                    if ds[0] == 2:
-                        rs1_copy(p, h, 0, k).start()
-                    elif ds[0]:
-                        rs1_copy(p, h, 1, k).start()
-
-    def pass_g(p, hs):
-        for h in hs:
-            for k in (0, 1):
-                rs1_copy(p, h, 0, k).wait_recv()
-                at = pl.ds(group_rows[h][sides[k]] + k * hg, hg)
-                g[p, at] = g[p, at] + rs1[p, h, k]
-                rs1_copy(p, h, 2, k).start()
+            for d in ds:
+                for h in hs:
+                    if d:
+                        rs1_copy(p, h, d).start()
 
     def mid_g(p, hs):
         for h in hs:
-            drain(g.at[p, pl.ds(0, 2 * group)], nf_r.at[p, h])
+            drain(g.at[p, pl.ds(0, (ring - 1) * group)], rs1_r.at[p, h])
             for e in far_first + [0]:
                 at = part_at(h, e)
-                s1[p, h, at] = g[p, chunk_at(h, e)] + near[p, h, at] + far[p, h, at]
+                total = g[p, chunk_at(h, e)]
+                for d in range(ring - 1):
+                    total = total + rs1[p, h, d, at]
+                s1[p, h, at] = total
                 if e:
                     rs2_copy(p, h, e).start()
 
@@ -238,8 +225,6 @@
             start_g(p, hs)
         for p in range(PARTS):
             drain(ur.at[p], rg_s.at[p])
-        for p, hs in both:
-            pass_g(p, hs)
         for p, hs in both:
             mid_g(p, hs)
         for p, hs in both:
@@ -317,9 +302,7 @@
             v((LANES, LANES), F32),
             v((QUARTERS, chunk, LANES), F32),
             v((PARTS, width, LANES), F32),
-            v(each + (2, group // 2, LANES), F32),
-            v(each + (group, LANES), F32),
-            v(each + (group, LANES), F32),
+            v(each + (ring - 1, group, LANES), F32),
             v(each + (group, LANES), F32),
             v(each + (ring - 1, chunk, LANES), F32),
             v((PARTS, width, LANES), BF16),
@@ -327,7 +310,7 @@
             v((PARTS, npeer, piece, LANES), BF16),
             v((PARTS, rows, LANES), BF16),
             dma((3 + PARTS,)),
-            dma(each + (2,)), dma(each), dma(each), dma((PARTS,)),
+            dma(each), dma(each), dma((PARTS,)),
             dma(each), dma(each), dma((PARTS,)),
             dma((PARTS,)), dma((PARTS,)), dma((PARTS,)), dma((PARTS,)),
             dma(each), dma(each + (2,)), dma(each), dma((PARTS,)),

time: 149 us -> 160 us (1.074)
  Pallas kernels: 146 us -> 157 us
    pallas_call x1, Pallas kernels: 146 us -> 157 us  [local_solve(): pl.pallas_call(functools.partial(ridge_kernel, ring, chips, samples, ridg...]
where the time goes in v5:
time: 160 us
  Pallas kernels  157 us (98%)
  local copies, waits for them, and re-layouts  2.11 us (1%)
    pallas_call x1, Pallas kernels, local_solve(): pl.pallas_call(functools.partial(ridge_kernel, ring, chips, samples, ridg...  157 us

profile of v5, /device:TPU:1, one launch (start us, length us, event | category | flops | bytes accessed | tf_op | source)
XLA Modules:
  0.0 159.7 jit_solution(11197377205643500691)
XLA Ops:
  0.6 156.9 %shard_map.59 = (f32[2048,256]{1,0:T(8,128)S(1)}, f32[512,256]{1,0:T(8,128)S(1)}) custom-call(bf16[512,2048]{1,0:T(8,128)(2,1)} %x_hbm.1, f32[2048,256]{1,0:T(8,128)} %w_hbm.1, f32[512,256]{1,0:T(8,128)} %y_hbm.1, f32[16,128]{1,0:T(8,128)} %bitcast.1), custom_call_target="tpu_custom_call" | custom-call | tf_op jit(solution)/shard_map/pallas_call | solution.py:319
  157.5 1.3 copy.8
  158.9 0.8 copy.9

commit v6 on v4

--- a/solution.py
+++ b/solution.py
@@ -21,7 +21,7 @@
 
 
 def ridge_kernel(ring, chips, samples, ridge, x_hbm, w_hbm, y_hbm, eta_hbm, wo, ro,
-                 x, xt, w_in, w, r, eta_in, eta_t, eta, g, rs1, near, far, s1, rs2, dw, u, ur, rb,
+                 x, xt, w_in, w, r, eta_in, eta_t, eta, g, rs1, near, far, s1, rs2, dw, acc, u, ur, rb,
                  load_sem, rl_r, nf_r, rs2_r, gs_s, ag1_r, ag3_r, ag_s,
                  u_s, u_r, rg_s, rg_r, wg1_r, wg2_r, wg3_r, wg_s, rf_s, rf_r):
     samp = lax.axis_index("samp")
@@ -128,11 +128,19 @@
     ag = Gather(lambda p, at: dw.at[p, at], ag1_r, None, ag3_r, ag_s)
     wg = Gather(lambda p, at: wo.at[at, columns(p)], wg1_r, wg2_r, wg3_r, wg_s)
 
-    def start_u(p):
+    def take_u(p, h, fresh):
         step = max(rows // 2, piece)
         for k in range(rows // step):
             at = pl.ds(k * step, step)
-            u[p, at] = jnp.dot(x[at], dw[p], preferred_element_type=F32).astype(BF16)
+            term = jnp.dot(x[at, h * quarter:(h + 1) * quarter], dw[p, h * quarter:(h + 1) * quarter], preferred_element_type=F32)
+            if not fresh:
+                term = acc[at] + term
+            if h == QUARTERS - 1:
+                u[p, at] = term.astype(BF16)
+            else:
+                acc[at] = term
+
+    def send_u(p):
         for i in range(len(peers)):
             u_copy(p, i).start()
 
@@ -214,10 +222,14 @@
         for h in everything:
             w[p, h] = w_in[chunk_at(h, 0), p * LANES:(p + 1) * LANES]
     loads[1].wait()
+    for p in range(PARTS):
+        step = max(rows // 2, piece)
+        for k in range(rows // step):
+            at = pl.ds(k * step, step)
+            u[p, at] = jnp.dot(x[at], dw[p], preferred_element_type=F32).astype(BF16)
     pl.semaphore_wait(barrier, 2 * (ring - 1) + len(peers))
-
-    for p in range(PARTS):
-        start_u(p)
+    for p in range(PARTS):
+        send_u(p)
     tile = min(width, 256)
     for k in range(width // tile):
         xt[k * tile:(k + 1) * tile] = x[:, k * tile:(k + 1) * tile].T
@@ -255,8 +267,9 @@
             drain(g.at[p, pl.ds(0, QUARTERS * (3 * group + (ring - 1) * chunk))], gs_s.at[p])
             for h in everything:
                 ag.last(p, h)
+                take_u(p, h, h == 0)
+            send_u(p)
             ag.sent(p)
-            start_u(p)
         if last:
             for p in range(PARTS):
                 for h in everything:
@@ -323,6 +336,7 @@
             v(each + (group, LANES), F32),
             v(each + (ring - 1, chunk, LANES), F32),
             v((PARTS, width, LANES), BF16),
+            v((rows, LANES), F32),
             v((PARTS, rows, LANES), BF16),
             v((PARTS, npeer, piece, LANES), BF16),
             v((PARTS, rows, LANES), BF16),

time: 149 us -> 150 us (level)
  no operation moved by 1% of the time
where the time goes in v6:
time: 150 us
  Pallas kernels  147 us (98%)
  local copies, waits for them, and re-layouts  2.11 us (1%)
    pallas_call x1, Pallas kernels, local_solve(): pl.pallas_call(functools.partial(ridge_kernel, ring, chips, samples, ridg...  147 us

profile of v6, /device:TPU:1, one launch (start us, length us, event | category | flops | bytes accessed | tf_op | source)
XLA Modules:
  0.0 149.6 jit_solution(1019137174735513180)
XLA Ops:
  0.6 146.8 %shard_map.59 = (f32[2048,256]{1,0:T(8,128)S(1)}, f32[512,256]{1,0:T(8,128)S(1)}) custom-call(bf16[512,2048]{1,0:T(8,128)(2,1)} %x_hbm.1, f32[2048,256]{1,0:T(8,128)} %w_hbm.1, f32[512,256]{1,0:T(8,128)} %y_hbm.1, f32[16,128]{1,0:T(8,128)} %bitcast.1), custom_call_target="tpu_custom_call" | custom-call | tf_op jit(solution)/shard_map/pallas_call | solution.py:350
  147.5 1.3 copy.8
  148.8 0.8 copy.9

commit v7 on v4

--- a/solution.py
+++ b/solution.py
@@ -128,11 +128,13 @@
     ag = Gather(lambda p, at: dw.at[p, at], ag1_r, None, ag3_r, ag_s)
     wg = Gather(lambda p, at: wo.at[at, columns(p)], wg1_r, wg2_r, wg3_r, wg_s)
 
-    def start_u(p):
+    def take_u(p):
         step = max(rows // 2, piece)
         for k in range(rows // step):
             at = pl.ds(k * step, step)
             u[p, at] = jnp.dot(x[at], dw[p], preferred_element_type=F32).astype(BF16)
+
+    def send_u(p):
         for i in range(len(peers)):
             u_copy(p, i).start()
 
@@ -214,10 +216,11 @@
         for h in everything:
             w[p, h] = w_in[chunk_at(h, 0), p * LANES:(p + 1) * LANES]
     loads[1].wait()
+    for p in range(PARTS):
+        take_u(p)
     pl.semaphore_wait(barrier, 2 * (ring - 1) + len(peers))
-
-    for p in range(PARTS):
-        start_u(p)
+    for p in range(PARTS):
+        send_u(p)
     tile = min(width, 256)
     for k in range(width // tile):
         xt[k * tile:(k + 1) * tile] = x[:, k * tile:(k + 1) * tile].T
@@ -255,8 +258,9 @@
             drain(g.at[p, pl.ds(0, QUARTERS * (3 * group + (ring - 1) * chunk))], gs_s.at[p])
             for h in everything:
                 ag.last(p, h)
+            take_u(p)
+            send_u(p)
             ag.sent(p)
-            start_u(p)
         if last:
             for p in range(PARTS):
                 for h in everything:

time: 149 us -> 150 us (level)
  no operation moved by 1% of the time
where the time goes in v7:
time: 150 us
  Pallas kernels  147 us (98%)
  local copies, waits for them, and re-layouts  2.11 us (1%)
    pallas_call x1, Pallas kernels, local_solve(): pl.pallas_call(functools.partial(ridge_kernel, ring, chips, samples, ridg...  147 us

profile of v7, /device:TPU:1, one launch (start us, length us, event | category | flops | bytes accessed | tf_op | source)
XLA Modules:
  0.0 150.1 jit_solution(4378180400391687786)
XLA Ops:
  0.6 147.4 %shard_map.59 = (f32[2048,256]{1,0:T(8,128)S(1)}, f32[512,256]{1,0:T(8,128)S(1)}) custom-call(bf16[512,2048]{1,0:T(8,128)(2,1)} %x_hbm.1, f32[2048,256]{1,0:T(8,128)} %w_hbm.1, f32[512,256]{1,0:T(8,128)} %y_hbm.1, f32[16,128]{1,0:T(8,128)} %bitcast.1), custom_call_target="tpu_custom_call" | custom-call | tf_op jit(solution)/shard_map/pallas_call | solution.py:340
  148.0 1.3 copy.8
  149.3 0.8 copy.9

commit v8 on v4

--- a/solution.py
+++ b/solution.py
@@ -13,8 +13,8 @@
 RIDGE_SCALE = 0.1
 PARTS = 2
 LANES = 128
-QUARTERS = 4
-UNITS = ((0, 1), (2, 3))
+QUARTERS = 2
+UNITS = ((0, 1),)
 MESH = pl.DeviceIdType.MESH
 F32 = jnp.float32
 BF16 = jnp.bfloat16

time: 149 us -> 156 us (1.047)
  Pallas kernels: 146 us -> 153 us
    pallas_call x1, Pallas kernels: 146 us -> 153 us  [local_solve(): pl.pallas_call(functools.partial(ridge_kernel, ring, chips, samples, ridg...]
where the time goes in v8:
time: 156 us
  Pallas kernels  153 us (98%)
  local copies, waits for them, and re-layouts  2.11 us (1%)
    pallas_call x1, Pallas kernels, local_solve(): pl.pallas_call(functools.partial(ridge_kernel, ring, chips, samples, ridg...  153 us

profile of v8, /device:TPU:1, one launch (start us, length us, event | category | flops | bytes accessed | tf_op | source)
XLA Modules:
  0.0 155.7 jit_solution(8292684867605420874)
XLA Ops:
  0.6 153.0 %shard_map.59 = (f32[2048,256]{1,0:T(8,128)S(1)}, f32[512,256]{1,0:T(8,128)S(1)}) custom-call(bf16[512,2048]{1,0:T(8,128)(2,1)} %x_hbm.1, f32[2048,256]{1,0:T(8,128)} %w_hbm.1, f32[512,256]{1,0:T(8,128)} %y_hbm.1, f32[16,128]{1,0:T(8,128)} %bitcast.1), custom_call_target="tpu_custom_call" | custom-call | tf_op jit(solution)/shard_map/pallas_call | solution.py:336
  153.6 1.3 copy.8
  154.9 0.8 copy.9

commit v9 on v8

--- a/solution.py
+++ b/solution.py
@@ -13,8 +13,8 @@
 RIDGE_SCALE = 0.1
 PARTS = 2
 LANES = 128
-QUARTERS = 2
-UNITS = ((0, 1),)
+QUARTERS = 8
+UNITS = ((0, 1), (2, 3), (4, 5), (6, 7))
 MESH = pl.DeviceIdType.MESH
 F32 = jnp.float32
 BF16 = jnp.bfloat16

time: 156 us -> 149 us (0.955)
  Pallas kernels: 153 us -> 146 us
    pallas_call x1, Pallas kernels: 153 us -> 146 us  [local_solve(): pl.pallas_call(functools.partial(ridge_kernel, ring, chips, samples, ridg...]
where the time goes in v9:
time: 149 us; the launch traced here: 148 us
  Pallas kernels  146 us (98%)
  local copies, waits for them, and re-layouts  2.11 us (1%)
    pallas_call x1, Pallas kernels, local_solve(): pl.pallas_call(functools.partial(ridge_kernel, ring, chips, samples, ridg...  146 us

profile of v9, /device:TPU:1, one launch (start us, length us, event | category | flops | bytes accessed | tf_op | source)
XLA Modules:
  0.0 148.4 jit_solution(15065902775495960053)
XLA Ops:
  0.6 145.7 %shard_map.59 = (f32[2048,256]{1,0:T(8,128)S(1)}, f32[512,256]{1,0:T(8,128)S(1)}) custom-call(bf16[512,2048]{1,0:T(8,128)(2,1)} %x_hbm.1, f32[2048,256]{1,0:T(8,128)} %w_hbm.1, f32[512,256]{1,0:T(8,128)} %y_hbm.1, f32[16,128]{1,0:T(8,128)} %bitcast.1), custom_call_target="tpu_custom_call" | custom-call | tf_op jit(solution)/shard_map/pallas_call | solution.py:336
  146.3 1.3 copy.8
  147.6 0.8 copy.9

commit v10 on v9

--- a/solution.py
+++ b/solution.py
@@ -152,17 +152,12 @@
     def start_g(p, hs):
         if hs == UNITS[0]:
             drain(ur.at[p], rg_r.at[p])
-        for ds in ((2,), (1, ring - 1), (0,)):
-            for d in ds:
-                for h in hs:
-                    at = group_at(h, d)
-                    g[p, at] = jnp.dot(xt[at], rb[p], preferred_element_type=F32)
+        at = slice(hs[0] * quarter, (hs[-1] + 1) * quarter)
+        g[p, at] = jnp.dot(xt[at], rb[p], preferred_element_type=F32)
+        for kind in (0, 1):
             for h in hs:
                 for k in (0, 1):
-                    if ds[0] == 2:
-                        rs1_copy(p, h, 0, k).start()
-                    elif ds[0]:
-                        rs1_copy(p, h, 1, k).start()
+                    rs1_copy(p, h, kind, k).start()
 
     def pass_g(p, hs):
         for h in hs:

time: 149 us -> 150 us (level)
  no operation moved by 1% of the time
where the time goes in v10:
time: 150 us; the launch traced here: 149 us
  Pallas kernels  147 us (98%)
  local copies, waits for them, and re-layouts  2.11 us (1%)
    pallas_call x1, Pallas kernels, local_solve(): pl.pallas_call(functools.partial(ridge_kernel, ring, chips, samples, ridg...  147 us

profile of v10, /device:TPU:1, one launch (start us, length us, event | category | flops | bytes accessed | tf_op | source)
XLA Modules:
  0.0 149.5 jit_solution(2384332552425725853)
XLA Ops:
  0.6 146.7 %shard_map.59 = (f32[2048,256]{1,0:T(8,128)S(1)}, f32[512,256]{1,0:T(8,128)S(1)}) custom-call(bf16[512,2048]{1,0:T(8,128)(2,1)} %x_hbm.1, f32[2048,256]{1,0:T(8,128)} %w_hbm.1, f32[512,256]{1,0:T(8,128)} %y_hbm.1, f32[16,128]{1,0:T(8,128)} %bitcast.1), custom_call_target="tpu_custom_call" | custom-call | tf_op jit(solution)/shard_map/pallas_call | solution.py:331
  147.3 1.3 copy.8
  148.7 0.8 copy.9

commit v11 on v10

--- a/solution.py
+++ b/solution.py
@@ -228,35 +228,27 @@
         send_r(p)
 
     def sweep(last):
-        both = [(p, hs) for p in range(PARTS) for hs in UNITS]
-        for p, hs in both:
-            start_g(p, hs)
-        for p in range(PARTS):
+        def first_g(p):
+            for hs in UNITS:
+                start_g(p, hs)
             drain(ur.at[p], rg_s.at[p])
-        for p, hs in both:
-            pass_g(p, hs)
-        for p, hs in both:
-            mid_g(p, hs)
-        for p, hs in both:
-            end_g(p, hs, last)
-        for p, hs in both:
-            for h in hs:
+
+        def each_unit(stage, p, *more):
+            for hs in UNITS:
+                stage(p, hs, *more)
+
+        def second(p):
+            for h in everything:
                 ag.second(p, h)
-        if last:
-            for p in range(PARTS):
-                for h in everything:
-                    wg.first(p, h)
-        for p in range(PARTS):
+
+        def finish(p):
             drain(g.at[p, pl.ds(0, QUARTERS * (3 * group + (ring - 1) * chunk))], gs_s.at[p])
             for h in everything:
                 ag.last(p, h)
             ag.sent(p)
             start_u(p)
-        if last:
-            for p in range(PARTS):
-                for h in everything:
-                    wg.second(p, h)
-        for p in range(PARTS):
+
+        def update(p):
             r[p] = r[p] - COMBINE_WEIGHT * sum_u(p)
             if last:
                 ro[mine, p * LANES:(p + 1) * LANES] = r[p]
@@ -264,6 +256,32 @@
                     r_copy(ro.at[mine, columns(p)], rf_s, rf_r, p, i).start()
             else:
                 send_r(p)
+
+        def start_w(p):
+            if last:
+                for h in everything:
+                    wg.first(p, h)
+
+        first_g(0)
+        each_unit(pass_g, 0)
+        first_g(1)
+        each_unit(mid_g, 0)
+        each_unit(pass_g, 1)
+        each_unit(end_g, 0, last)
+        each_unit(mid_g, 1)
+        second(0)
+        each_unit(end_g, 1, last)
+        start_w(0)
+        finish(0)
+        second(1)
+        start_w(1)
+        update(0)
+        finish(1)
+        if last:
+            for p in range(PARTS):
+                for h in everything:
+                    wg.second(p, h)
+        update(1)
         if last:
             for p in range(PARTS):
                 for h in everything:

time: 150 us -> 152 us (1.013)
  Pallas kernels: 147 us -> 149 us
    pallas_call x1, Pallas kernels: 147 us -> 149 us  [local_solve(): pl.pallas_call(functools.partial(ridge_kernel, ring, chips, samples, ridg...]
where the time goes in v11:
time: 152 us
  Pallas kernels  149 us (98%)
  local copies, waits for them, and re-layouts  2.11 us (1%)
    pallas_call x1, Pallas kernels, local_solve(): pl.pallas_call(functools.partial(ridge_kernel, ring, chips, samples, ridg...  149 us

profile of v11, /device:TPU:1, one launch (start us, length us, event | category | flops | bytes accessed | tf_op | source)
XLA Modules:
  0.0 152.1 jit_solution(8783746327263656646)
XLA Ops:
  0.6 149.3 %shard_map.59 = (f32[2048,256]{1,0:T(8,128)S(1)}, f32[512,256]{1,0:T(8,128)S(1)}) custom-call(bf16[512,2048]{1,0:T(8,128)(2,1)} %x_hbm.1, f32[2048,256]{1,0:T(8,128)} %w_hbm.1, f32[512,256]{1,0:T(8,128)} %y_hbm.1, f32[16,128]{1,0:T(8,128)} %bitcast.1), custom_call_target="tpu_custom_call" | custom-call | tf_op jit(solution)/shard_map/pallas_call | solution.py:349
  150.0 1.3 copy.8
  151.3 0.8 copy.9

commit v12 on v9

--- a/solution.py
+++ b/solution.py
@@ -13,6 +13,7 @@
 RIDGE_SCALE = 0.1
 PARTS = 2
 LANES = 128
+STORES = 4
 QUARTERS = 8
 UNITS = ((0, 1), (2, 3), (4, 5), (6, 7))
 MESH = pl.DeviceIdType.MESH
@@ -128,11 +129,13 @@
     ag = Gather(lambda p, at: dw.at[p, at], ag1_r, None, ag3_r, ag_s)
     wg = Gather(lambda p, at: wo.at[at, columns(p)], wg1_r, wg2_r, wg3_r, wg_s)
 
-    def start_u(p):
+    def take_u(p):
         step = max(rows // 2, piece)
         for k in range(rows // step):
             at = pl.ds(k * step, step)
             u[p, at] = jnp.dot(x[at], dw[p], preferred_element_type=F32).astype(BF16)
+
+    def send_u(p):
         for i in range(len(peers)):
             u_copy(p, i).start()
 
@@ -214,10 +217,12 @@
         for h in everything:
             w[p, h] = w_in[chunk_at(h, 0), p * LANES:(p + 1) * LANES]
     loads[1].wait()
+    take_u(0)
     pl.semaphore_wait(barrier, 2 * (ring - 1) + len(peers))
-
-    for p in range(PARTS):
-        start_u(p)
+    send_u(0)
+    for p in range(1, PARTS):
+        take_u(p)
+        send_u(p)
     tile = min(width, 256)
     for k in range(width // tile):
         xt[k * tile:(k + 1) * tile] = x[:, k * tile:(k + 1) * tile].T
@@ -256,7 +261,8 @@
             for h in everything:
                 ag.last(p, h)
             ag.sent(p)
-            start_u(p)
+            take_u(p)
+            send_u(p)
         if last:
             for p in range(PARTS):
                 for h in everything:
@@ -288,6 +294,16 @@
         for h in everything:
             wg.last(p, h)
         wg.sent(p)
+
+
+def store_kernel(w_in, r_in, w_out, r_out, sem):
+    rows = w_in.shape[0] // STORES
+    stores = [pltpu.make_async_copy(w_in.at[pl.ds(k * rows, rows)], w_out.at[pl.ds(k * rows, rows)], sem.at[k]) for k in range(STORES)]
+    stores.append(pltpu.make_async_copy(r_in, r_out, sem.at[STORES]))
+    for store in stores:
+        store.start()
+    for store in stores:
+        store.wait()
 
 
 def solution(mesh):
@@ -333,7 +349,7 @@
             dma(each), dma(each + (2,)), dma(each), dma((PARTS,)),
             dma((PARTS,)), dma((PARTS,)),
         ]
-        return pl.pallas_call(
+        solved = pl.pallas_call(
             functools.partial(ridge_kernel, ring, chips, samples, ridge),
             out_shape=[pltpu.VMEM(w_loc.shape, F32), pltpu.VMEM(y_loc.shape, F32)],
             in_specs=[pl.BlockSpec(memory_space=pltpu.HBM)] * 4,
@@ -342,6 +358,14 @@
             compiler_params=pltpu.CompilerParams(
                 collective_id=0, has_side_effects=True, vmem_limit_bytes=56 * 1024 * 1024),
         )(x_loc, w_loc, y_loc, eta_loc.reshape(width // LANES, LANES))
+        return pl.pallas_call(
+            store_kernel,
+            out_shape=[jax.ShapeDtypeStruct(w_loc.shape, F32), jax.ShapeDtypeStruct(y_loc.shape, F32)],
+            in_specs=[pl.BlockSpec(memory_space=pltpu.VMEM)] * 2,
+            out_specs=[pl.BlockSpec(memory_space=pltpu.HBM)] * 2,
+            scratch_shapes=[dma((STORES + 1,))],
+            compiler_params=pltpu.CompilerParams(vmem_limit_bytes=4 * 1024 * 1024),
+        )(*solved)
 
     return jax.shard_map(
         local_solve,

time: 149 us -> 148 us (level)
  local copies, waits for them, and re-layouts: 2.11 us -> 0 us
    unnamed x2 -> x0, local copies, waits for them, and re-layouts: 2.11 us -> none
    pallas_call x0 -> x1, Pallas kernels: none -> 1.53 us  [local_solve(): pl.pallas_call(store_kernel, out_shape=[jax.ShapeDtypeStruct(w_loc.shape,...]
where the time goes in v12:
time: 148 us; the launch traced here: 147 us
  Pallas kernels  147 us (99%)
    pallas_call x1, Pallas kernels, local_solve(): pl.pallas_call(functools.partial(ridge_kernel, ring, chips, samples, ridg...  145 us

profile of v12, /device:TPU:1, one launch (start us, length us, event | category | flops | bytes accessed | tf_op | source)
XLA Modules:
  0.0 147.5 jit_solution(8278032117692370618)
XLA Ops:
  0.6 145.3 %shard_map.59 = (f32[2048,256]{1,0:T(8,128)S(1)}, f32[512,256]{1,0:T(8,128)S(1)}) custom-call(bf16[512,2048]{1,0:T(8,128)(2,1)} %x_hbm.1, f32[2048,256]{1,0:T(8,128)} %w_hbm.1, f32[512,256]{1,0:T(8,128)} %y_hbm.1, f32[16,128]{1,0:T(8,128)} %bitcast.1), custom_call_target="tpu_custom_call" | custom-call | tf_op jit(solution)/shard_map/pallas_call | solution.py:352
  146.0 1.5 %shard_map.60 = (f32[2048,256]{1,0:T(8,128)}, f32[512,256]{1,0:T(8,128)}) custom-call(f32[2048,256]{1,0:T(8,128)S(1)} %get-tuple-element.4.w_in, f32[512,256]{1,0:T(8,128)S(1)} %get-tuple-element.5.r_in), custom_call_target="tpu_custom_call" | custom-call | tf_op jit(solution)/shard_map/pallas_call | solution.py:361

commit v13 on v12

--- a/solution.py
+++ b/solution.py
@@ -155,17 +155,16 @@
     def start_g(p, hs):
         if hs == UNITS[0]:
             drain(ur.at[p], rg_r.at[p])
-        for ds in ((2,), (1, ring - 1), (0,)):
-            for d in ds:
-                for h in hs:
-                    at = group_at(h, d)
-                    g[p, at] = jnp.dot(xt[at], rb[p], preferred_element_type=F32)
-            for h in hs:
-                for k in (0, 1):
-                    if ds[0] == 2:
-                        rs1_copy(p, h, 0, k).start()
-                    elif ds[0]:
-                        rs1_copy(p, h, 1, k).start()
+        at = slice(hs[0] * quarter, (hs[-1] + 1) * quarter)
+        g[p, at] = jnp.dot(xt[at], rb[p], preferred_element_type=F32)
+        send_g(p, hs, 0)
+        if p == 0:
+            send_g(p, hs, 1)
+
+    def send_g(p, hs, kind):
+        for h in hs:
+            for k in (0, 1):
+                rs1_copy(p, h, kind, k).start()
 
     def pass_g(p, hs):
         for h in hs:
@@ -245,6 +244,9 @@
             drain(ur.at[p], rg_s.at[p])
         for p, hs in both:
             pass_g(p, hs)
+            if p == 0:
+                for q in range(1, PARTS):
+                    send_g(q, hs, 1)
         for p, hs in both:
             mid_g(p, hs)
         for p, hs in both:

time: 148 us -> 147 us (level)
  no operation moved by 1% of the time
where the time goes in v13:
time: 147 us
  Pallas kernels  147 us (100%)
    pallas_call x1, Pallas kernels, local_solve(): pl.pallas_call(functools.partial(ridge_kernel, ring, chips, samples, ridg...  145 us

profile of v13, /device:TPU:1, one launch (start us, length us, event | category | flops | bytes accessed | tf_op | source)
XLA Modules:
  0.0 147.3 jit_solution(8557946110182100872)
XLA Ops:
  0.6 145.2 %shard_map.59 = (f32[2048,256]{1,0:T(8,128)S(1)}, f32[512,256]{1,0:T(8,128)S(1)}) custom-call(bf16[512,2048]{1,0:T(8,128)(2,1)} %x_hbm.1, f32[2048,256]{1,0:T(8,128)} %w_hbm.1, f32[512,256]{1,0:T(8,128)} %y_hbm.1, f32[16,128]{1,0:T(8,128)} %bitcast.1), custom_call_target="tpu_custom_call" | custom-call | tf_op jit(solution)/shard_map/pallas_call | solution.py:354
  145.8 1.5 %shard_map.60 = (f32[2048,256]{1,0:T(8,128)}, f32[512,256]{1,0:T(8,128)}) custom-call(f32[2048,256]{1,0:T(8,128)S(1)} %get-tuple-element.4.w_in, f32[512,256]{1,0:T(8,128)S(1)} %get-tuple-element.5.r_in), custom_call_target="tpu_custom_call" | custom-call | tf_op jit(solution)/shard_map/pallas_call | solution.py:363

commit v14 on v13

--- a/solution.py
+++ b/solution.py
@@ -39,7 +39,6 @@
     zs = [cz] + [lax.rem(cz + d, ring) for d in range(1, ring)]
     neighbour = [[cz * ring + c for c in ys], [c * ring + cy for c in zs]]
     far_first = sorted(range(1, ring), key=lambda d: -min(d, ring - d))
-    near_first = far_first[::-1]
     sides = (1, ring - 1)
     across = sorted(range(1, chips), key=lambda d: -min(d, chips - d))
     peers = [(dx, dc) for dx in across + [0] for dc in (0, 1) if dx or dc]
@@ -101,7 +100,7 @@
 
         def first(self, p, h):
             ref = self.view(p, chunk_at(h, 0))
-            for d in near_first:
+            for d in far_first:
                 remote(ref, ref, self.s.at[p], self.r1.at[p, h], along(h + 1, d)).start()
 
         def second(self, p, h):
@@ -129,15 +128,16 @@
     ag = Gather(lambda p, at: dw.at[p, at], ag1_r, None, ag3_r, ag_s)
     wg = Gather(lambda p, at: wo.at[at, columns(p)], wg1_r, wg2_r, wg3_r, wg_s)
 
-    def take_u(p):
-        step = max(rows // 2, piece)
-        for k in range(rows // step):
-            at = pl.ds(k * step, step)
-            u[p, at] = jnp.dot(x[at], dw[p], preferred_element_type=F32).astype(BF16)
-
-    def send_u(p):
-        for i in range(len(peers)):
-            u_copy(p, i).start()
+    def take_u(p, k):
+        step = rows // 2
+        side = lax.div(cx, chips // 2)
+        at = pl.ds((1 - side if k == 0 else side) * step, step)
+        u[p, at] = jnp.dot(x[at], dw[p], preferred_element_type=F32).astype(BF16)
+
+    def send_u(p, k):
+        for i, (dx, dc) in enumerate(peers):
+            if (dx == chips // 2) == (k == 0):
+                u_copy(p, i).start()
 
     def sum_u(p):
         total = u[p, mine].astype(F32)
@@ -216,12 +216,15 @@
         for h in everything:
             w[p, h] = w_in[chunk_at(h, 0), p * LANES:(p + 1) * LANES]
     loads[1].wait()
-    take_u(0)
+    for k in (0, 1):
+        take_u(0, k)
     pl.semaphore_wait(barrier, 2 * (ring - 1) + len(peers))
-    send_u(0)
+    for k in (0, 1):
+        send_u(0, k)
     for p in range(1, PARTS):
-        take_u(p)
-        send_u(p)
+        for k in (0, 1):
+            take_u(p, k)
+            send_u(p, k)
     tile = min(width, 256)
     for k in range(width // tile):
         xt[k * tile:(k + 1) * tile] = x[:, k * tile:(k + 1) * tile].T
@@ -262,9 +265,10 @@
             drain(g.at[p, pl.ds(0, QUARTERS * (3 * group + (ring - 1) * chunk))], gs_s.at[p])
             for h in everything:
                 ag.last(p, h)
+            for k in (0, 1):
+                take_u(p, k)
+                send_u(p, k)
             ag.sent(p)
-            take_u(p)
-            send_u(p)
         if last:
             for p in range(PARTS):
                 for h in everything:

time: 147 us -> 147 us (level)
  Pallas kernels: 147 us -> 145 us
where the time goes in v14:
time: 147 us; the launch traced here: 146 us
  Pallas kernels  145 us (99%)
    pallas_call x1, Pallas kernels, local_solve(): pl.pallas_call(functools.partial(ridge_kernel, ring, chips, samples, ridg...  144 us

profile of v14, /device:TPU:1, one launch (start us, length us, event | category | flops | bytes accessed | tf_op | source)
XLA Modules:
  0.0 146.1 jit_solution(9404307659370171698)
XLA Ops:
  0.6 144.0 %shard_map.59 = (f32[2048,256]{1,0:T(8,128)S(1)}, f32[512,256]{1,0:T(8,128)S(1)}) custom-call(bf16[512,2048]{1,0:T(8,128)(2,1)} %x_hbm.1, f32[2048,256]{1,0:T(8,128)} %w_hbm.1, f32[512,256]{1,0:T(8,128)} %y_hbm.1, f32[16,128]{1,0:T(8,128)} %bitcast.1), custom_call_target="tpu_custom_call" | custom-call | tf_op jit(solution)/shard_map/pallas_call | solution.py:358
  144.6 1.5 %shard_map.60 = (f32[2048,256]{1,0:T(8,128)}, f32[512,256]{1,0:T(8,128)}) custom-call(f32[2048,256]{1,0:T(8,128)S(1)} %get-tuple-element.4.w_in, f32[512,256]{1,0:T(8,128)S(1)} %get-tuple-element.5.r_in), custom_call_target="tpu_custom_call" | custom-call | tf_op jit(solution)/shard_map/pallas_call | solution.py:367

commit v15 on v14

--- a/solution.py
+++ b/solution.py
@@ -15,7 +15,7 @@
 LANES = 128
 STORES = 4
 QUARTERS = 8
-UNITS = ((0, 1), (2, 3), (4, 5), (6, 7))
+UNITS = tuple((h,) for h in range(QUARTERS))
 MESH = pl.DeviceIdType.MESH
 F32 = jnp.float32
 BF16 = jnp.bfloat16

time: 147 us -> 145 us (0.986)
  no operation moved by 1% of the time
where the time goes in v15:
time: 145 us
  Pallas kernels  144 us (99%)
    pallas_call x1, Pallas kernels, local_solve(): pl.pallas_call(functools.partial(ridge_kernel, ring, chips, samples, ridg...  143 us

profile of v15, /device:TPU:1, one launch (start us, length us, event | category | flops | bytes accessed | tf_op | source)
XLA Modules:
  0.0 145.0 jit_solution(3634249152509491058)
XLA Ops:
  0.6 142.8 %shard_map.59 = (f32[2048,256]{1,0:T(8,128)S(1)}, f32[512,256]{1,0:T(8,128)S(1)}) custom-call(bf16[512,2048]{1,0:T(8,128)(2,1)} %x_hbm.1, f32[2048,256]{1,0:T(8,128)} %w_hbm.1, f32[512,256]{1,0:T(8,128)} %y_hbm.1, f32[16,128]{1,0:T(8,128)} %bitcast.1), custom_call_target="tpu_custom_call" | custom-call | tf_op jit(solution)/shard_map/pallas_call | solution.py:358
  143.5 1.5 %shard_map.60 = (f32[2048,256]{1,0:T(8,128)}, f32[512,256]{1,0:T(8,128)}) custom-call(f32[2048,256]{1,0:T(8,128)S(1)} %get-tuple-element.4.w_in, f32[512,256]{1,0:T(8,128)S(1)} %get-tuple-element.5.r_in), custom_call_target="tpu_custom_call" | custom-call | tf_op jit(solution)/shard_map/pallas_call | solution.py:367

commit v16 on v15

--- a/solution.py
+++ b/solution.py
@@ -158,8 +158,9 @@
         at = slice(hs[0] * quarter, (hs[-1] + 1) * quarter)
         g[p, at] = jnp.dot(xt[at], rb[p], preferred_element_type=F32)
         send_g(p, hs, 0)
-        if p == 0:
-            send_g(p, hs, 1)
+        if p == 0 and hs == UNITS[-1]:
+            for each in UNITS:
+                send_g(p, each, 1)
 
     def send_g(p, hs, kind):
         for h in hs:

time: 145 us -> 148 us (1.021); the launches traced: 145 us -> 146 us
  Pallas kernels: 144 us -> 146 us
where the time goes in v16:
time: 148 us; the launch traced here: 146 us
  Pallas kernels  146 us (99%)
    pallas_call x1, Pallas kernels, local_solve(): pl.pallas_call(functools.partial(ridge_kernel, ring, chips, samples, ridg...  144 us

profile of v16, /device:TPU:1, one launch (start us, length us, event | category | flops | bytes accessed | tf_op | source)
XLA Modules:
  0.0 146.3 jit_solution(8690188575083589837)
XLA Ops:
  0.6 144.2 %shard_map.59 = (f32[2048,256]{1,0:T(8,128)S(1)}, f32[512,256]{1,0:T(8,128)S(1)}) custom-call(bf16[512,2048]{1,0:T(8,128)(2,1)} %x_hbm.1, f32[2048,256]{1,0:T(8,128)} %w_hbm.1, f32[512,256]{1,0:T(8,128)} %y_hbm.1, f32[16,128]{1,0:T(8,128)} %bitcast.1), custom_call_target="tpu_custom_call" | custom-call | tf_op jit(solution)/shard_map/pallas_call | solution.py:359
  144.8 1.5 %shard_map.60 = (f32[2048,256]{1,0:T(8,128)}, f32[512,256]{1,0:T(8,128)}) custom-call(f32[2048,256]{1,0:T(8,128)S(1)} %get-tuple-element.4.w_in, f32[512,256]{1,0:T(8,128)S(1)} %get-tuple-element.5.r_in), custom_call_target="tpu_custom_call" | custom-call | tf_op jit(solution)/shard_map/pallas_call | solution.py:368

commit v17 on v15

--- a/solution.py
+++ b/solution.py
@@ -158,8 +158,7 @@
         at = slice(hs[0] * quarter, (hs[-1] + 1) * quarter)
         g[p, at] = jnp.dot(xt[at], rb[p], preferred_element_type=F32)
         send_g(p, hs, 0)
-        if p == 0:
-            send_g(p, hs, 1)
+        send_g(p, hs, 1)
 
     def send_g(p, hs, kind):
         for h in hs:
@@ -247,9 +246,6 @@
             drain(ur.at[p], rg_s.at[p])
         for p, hs in both:
             pass_g(p, hs)
-            if p == 0:
-                for q in range(1, PARTS):
-                    send_g(q, hs, 1)
         for p, hs in both:
             mid_g(p, hs)
         for p, hs in both:

time: 145 us -> 149 us (1.028)
  Pallas kernels: 144 us -> 148 us
    pallas_call x1, Pallas kernels: 143 us -> 146 us  [local_solve(): pl.pallas_call(functools.partial(ridge_kernel, ring, chips, samples, ridg...]
where the time goes in v17:
time: 149 us; the launch traced here: 148 us
  Pallas kernels  148 us (99%)
    pallas_call x1, Pallas kernels, local_solve(): pl.pallas_call(functools.partial(ridge_kernel, ring, chips, samples, ridg...  146 us

profile of v17, /device:TPU:1, one launch (start us, length us, event | category | flops | bytes accessed | tf_op | source)
XLA Modules:
  0.0 148.4 jit_solution(9713491289024539890)
XLA Ops:
  0.6 146.3 %shard_map.59 = (f32[2048,256]{1,0:T(8,128)S(1)}, f32[512,256]{1,0:T(8,128)S(1)}) custom-call(bf16[512,2048]{1,0:T(8,128)(2,1)} %x_hbm.1, f32[2048,256]{1,0:T(8,128)} %w_hbm.1, f32[512,256]{1,0:T(8,128)} %y_hbm.1, f32[16,128]{1,0:T(8,128)} %bitcast.1), custom_call_target="tpu_custom_call" | custom-call | tf_op jit(solution)/shard_map/pallas_call | solution.py:354
  146.9 1.5 %shard_map.60 = (f32[2048,256]{1,0:T(8,128)}, f32[512,256]{1,0:T(8,128)}) custom-call(f32[2048,256]{1,0:T(8,128)S(1)} %get-tuple-element.4.w_in, f32[512,256]{1,0:T(8,128)S(1)} %get-tuple-element.5.r_in), custom_call_target="tpu_custom_call" | custom-call | tf_op jit(solution)/shard_map/pallas_call | solution.py:363
